TPU v7x, 128 devices: a whole 4x4x4 slice. The times are simulated.
128 devices in a mesh: dp: 16 (over x_lo, z, core), tensor: 8 (over y, x_hi).
Axes of the slice: x: 4 (x_hi: 2, x_lo: 2; x = x_hi * 2 + x_lo), y: 4, z: 4, core: 2. Of those that a mesh axis runs over, the one named last changes fastest.
Arguments:
- token_ids: int32 [16, 1024], P('dp', 'tensor'), may hold values from 0 to 30527
- lengths: int32 [16], P('dp'), may hold values from 256 to 1024, as said below
- teacher_bins: int32 [16], P('dp'), may hold values from 0 to 127
- embed_table: bfloat16 [30528, 1024], P('tensor'), may hold values from -6 to 6
- query_key_value_matrix: bfloat16 [1024, 3, 1024], P('dp', None, 'tensor'), may hold values from -2 to 2
- output_matrix: bfloat16 [1024, 1024], P('tensor', 'dp'), may hold values from -0.1875 to 0.1875
- up_matrix: bfloat16 [1024, 4096], P('dp', 'tensor'), may hold values from -0.1875 to 0.1875
- down_matrix: bfloat16 [4096, 1024], P('tensor', 'dp'), may hold values from -0.09375 to 0.09375
- w_head: bfloat16 [1024, 128], P('dp'), may hold values from -64 to 64
Outputs:
- loss: float32 [], replicated
- query_key_value_gradient: float32 [1024, 3, 1024], P('dp', None, 'tensor')
- output_weight_gradient: float32 [1024, 1024], P('tensor', 'dp')
- up_weight_gradient: float32 [1024, 4096], P('dp', 'tensor')
- down_weight_gradient: float32 [4096, 1024], P('tensor', 'dp')
- grad_head: float32 [1024, 128], P('dp')
Inputs may be any that keep to these rules, and one draw needn't show every extreme that they name: lengths[0] is 1024.
All inputs are finite; a program needn't handle non-finite values.
Results may differ from a plain program's by a relative error of at most 0.02.
Values may be sent and summed in bfloat16 or wider, within the bound.
A program may use at most 128 MiB of HBM per device.

v0:
```python
import functools

import jax
import jax.numpy as jnp
from jax import lax
from jax.experimental import pallas as pl
from jax.experimental.pallas import tpu as pltpu
from jax.sharding import Mesh
from jax.sharding import PartitionSpec as P

MESH = pl.DeviceIdType.MESH
EPS = 1e-05
F32 = jnp.float32
BF16 = jnp.bfloat16
HIGH = lax.Precision.HIGHEST
VM = pl.BlockSpec(memory_space=pltpu.VMEM)
SM = pl.BlockSpec(memory_space=pltpu.SMEM)


def where_am_i():
    return {name: lax.axis_index(name) for name in ("xl", "z", "c", "y", "xh")}


def add_mod(value, step, size):
    return lax.rem(value + step, size)


def params(number):
    return pltpu.CompilerParams(collective_id=number, has_side_effects=True)


def remote(src, dst, send, recv, device):
    return pltpu.make_async_remote_copy(
        src_ref=src, dst_ref=dst, send_sem=send, recv_sem=recv, device_id=device, device_id_type=MESH
    )


def signal(device):
    pl.semaphore_signal(pltpu.get_barrier_semaphore(), inc=1, device_id=device, device_id_type=MESH)


def normalize(values):
    mean = jnp.mean(values, axis=-1, keepdims=True)
    centered = values - mean
    return centered * lax.rsqrt(jnp.mean(centered * centered, axis=-1, keepdims=True) + EPS)


def normalize_back(values, grad):
    mean = jnp.mean(values, axis=-1, keepdims=True)
    centered = values - mean
    scale = lax.rsqrt(jnp.mean(centered * centered, axis=-1, keepdims=True) + EPS)
    normed = centered * scale
    return scale * (
        grad
        - jnp.mean(grad, axis=-1, keepdims=True)
        - normed * jnp.mean(grad * normed, axis=-1, keepdims=True)
    )


def spread_ids_kernel(src, out, send, recv):
    me = where_am_i()
    xl, z, c, y, xh = (me[n] for n in ("xl", "z", "c", "y", "xh"))
    here = xh == c

    for role in range(2):
        for k in range(4):
            source = dict(
                xl=add_mod(xl, role, 2), c=add_mod(xh, role, 2), xh=c, y=add_mod(y, 4 - k, 4), z=z
            )
            if role == 0 and k == 0:

                @pl.when(jnp.logical_not(here))
                def _(source=source):
                    signal(source)
            else:
                signal(source)
    pl.semaphore_wait(pltpu.get_barrier_semaphore(), jnp.where(here, 7, 8))

    def copy(role, k):
        return remote(
            src,
            out.at[role, y],
            send.at[role, k],
            recv.at[role, k],
            dict(xl=add_mod(xl, role, 2), c=xh, xh=add_mod(c, role, 2), y=add_mod(y, k, 4), z=z),
        )

    for role in range(2):
        for k in range(4):
            if role == 0 and k == 0:

                @pl.when(jnp.logical_not(here))
                def _():
                    copy(0, 0).start()

                @pl.when(here)
                def _():
                    pltpu.make_async_copy(src, out.at[0, y], recv.at[0, 0]).start()
            else:
                copy(role, k).start()
    for role in range(2):
        for k in range(4):
            if role == 0 and k == 0:

                @pl.when(jnp.logical_not(here))
                def _():
                    copy(0, 0).wait_send()
            else:
                copy(role, k).wait_send()
            pltpu.make_async_copy(src, out.at[role, add_mod(y, 4 - k, 4)], recv.at[role, k]).wait()


def spread_ids(packet):
    return pl.pallas_call(
        spread_ids_kernel,
        out_shape=jax.ShapeDtypeStruct((2, 4, 8, 128), jnp.int32),
        in_specs=[VM],
        out_specs=VM,
        scratch_shapes=[pltpu.SemaphoreType.DMA((2, 4)), pltpu.SemaphoreType.DMA((2, 4))],
        compiler_params=params(1),
        name="spread_ids",
    )(packet)


def plane_kernel(count, collect, *refs):
    me = where_am_i()
    xl, z, c, y, xh = (me[n] for n in ("xl", "z", "c", "y", "xh"))
    here = xh == c
    srcs, dsts = refs[:count], refs[count : 2 * count]
    send, recv = refs[2 * count :]
    mine, other = (xh, c) if collect else (c, xh)

    def target(a, k, e):
        swapped = dict(c=e, xh=c) if collect else dict(c=xh, xh=e)
        return dict(xl=add_mod(xl, a, 2), z=add_mod(z, k, 4), y=y, **swapped)

    def origin(a, k, e):
        swapped = dict(c=xh, xh=e) if collect else dict(c=e, xh=c)
        return dict(xl=add_mod(xl, a, 2), z=add_mod(z, 4 - k, 4), y=y, **swapped)

    def number(a, k, e, back):
        return (add_mod(xl, a, 2) * 4 + add_mod(z, 4 - k if back else k, 4)) * 2 + e

    slot = (xl * 4 + z) * 2 + mine

    def block(i, a, k, e):
        if collect and len(srcs[i].shape) == 3 and srcs[i].shape[0] == 16:
            return srcs[i].at[number(a, k, e, False)]
        return srcs[i]

    def copy(i, a, k, e):
        return remote(
            block(i, a, k, e),
            dsts[i].at[slot],
            send.at[i, a, k, e],
            recv.at[i, a, k, mine],
            target(a, k, e),
        )

    places = [(a, k, e) for k in (1, 3, 2, 0) for a in (1, 0) for e in range(2)]

    def is_self(a, k, e):
        return jnp.logical_and(here, e == other)

    for a, k, e in places:
        if a == 0 and k == 0:
            @pl.when(jnp.logical_not(jnp.logical_and(here, e == mine)))
            def _(a=a, k=k, e=e):
                signal(origin(a, k, e))
        else:
            signal(origin(a, k, e))
    pl.semaphore_wait(pltpu.get_barrier_semaphore(), jnp.where(here, 15, 16))
    for i in range(count):
        for a, k, e in places:
            if a == 0 and k == 0:

                @pl.when(jnp.logical_not(is_self(a, k, e)))
                def _(i=i, a=a, k=k, e=e):
                    copy(i, a, k, e).start()

                @pl.when(is_self(a, k, e))
                def _(i=i, a=a, k=k, e=e):
                    pltpu.make_async_copy(
                        block(i, a, k, e), dsts[i].at[slot], recv.at[i, a, k, mine]
                    ).start()
            else:
                copy(i, a, k, e).start()

    def finish(i):
        for a, k, e in places:
            if a == 0 and k == 0:

                @pl.when(jnp.logical_not(is_self(a, k, e)))
                def _(a=a, k=k, e=e):
                    copy(i, a, k, e).wait_send()
            else:
                copy(i, a, k, e).wait_send()
            pltpu.make_async_copy(
                block(i, 0, 0, 0), dsts[i].at[number(a, k, e, True)], recv.at[i, a, k, e]
            ).wait()

    return finish


def spread_kernel(count, *refs):
    finish = plane_kernel(count, False, *refs)
    for i in range(count):
        finish(i)


def spread(shards):
    count = len(shards)
    return pl.pallas_call(
        functools.partial(spread_kernel, count),
        out_shape=[jax.ShapeDtypeStruct((16, *s.shape), s.dtype) for s in shards],
        in_specs=[VM] * count,
        out_specs=[VM] * count,
        scratch_shapes=[pltpu.SemaphoreType.DMA((count, 2, 4, 2))] * 2,
        compiler_params=params(2),
        name="spread_weights",
    )(*shards)


def collect_kernel(count, *refs):
    ins, outs = refs[:count], refs[count : 2 * count]
    bufs = refs[2 * count : 3 * count - 1]
    sems = refs[3 * count - 1 :]
    finish = plane_kernel(count, True, *ins, outs[0], *bufs, *sems)
    finish(0)
    for i in range(1, count):
        finish(i)
        total = bufs[i - 1][0].astype(F32)
        for s in range(1, 16):
            total = total + bufs[i - 1][s].astype(F32)
        outs[i][...] = total


def collect(packet, grads):
    count = 1 + len(grads)
    shapes = [jax.ShapeDtypeStruct((16, *packet.shape), packet.dtype)]
    shapes += [jax.ShapeDtypeStruct(g.shape[1:], F32) for g in grads]
    return pl.pallas_call(
        functools.partial(collect_kernel, count),
        out_shape=shapes,
        in_specs=[VM] * count,
        out_specs=[VM] * count,
        scratch_shapes=[pltpu.VMEM(g.shape, g.dtype) for g in grads]
        + [pltpu.SemaphoreType.DMA((count, 2, 4, 2))] * 2,
        compiler_params=params(3),
        name="collect_gradients",
    )(packet, *grads)


def ring_places():
    me = where_am_i()
    y, c = me["y"], me["c"]
    return me, y, c, add_mod(y, 1, 4), add_mod(y, 3, 4), add_mod(y, 2, 4), 1 - c


HALVES = (pl.ds(0, 64), pl.ds(64, 64))


def to_owner(blocks, stage, far, near, send, recv):
    me, y, c, up, dn, op, oc = ring_places()
    first = [
        remote(blocks(op).at[HALVES[0]], far.at[0], send.at[0], recv.at[0], dict(y=up)),
        remote(blocks(op).at[HALVES[1]], far.at[1], send.at[1], recv.at[1], dict(y=dn)),
    ]
    for step in first:
        step.start()

    def second(side):
        return remote(
            stage.at[side], near.at[side], send.at[2 + side], recv.at[2 + side], dict(y=(up, dn)[side])
        )

    stage[0, 64:128] = blocks(up)[64:128]
    stage[1, 0:64] = blocks(dn)[0:64]
    first[0].wait_recv()
    stage[0, 0:64] = (blocks(up)[0:64].astype(F32) + far[0].astype(F32)).astype(BF16)
    second(0).start()
    first[1].wait_recv()
    stage[1, 64:128] = (blocks(dn)[64:128].astype(F32) + far[1].astype(F32)).astype(BF16)
    second(1).start()

    def finish():
        for step in first:
            step.wait_send()
        second(0).wait()
        second(1).wait()
        return blocks(y)[...].astype(F32) + near[0].astype(F32) + near[1].astype(F32)

    return finish


def to_all(out, send, recv):
    me, y, c, up, dn, op, oc = ring_places()

    def go(k, row, col, part, device):
        ref = out.at[row, col] if part is None else out.at[row, col, HALVES[part]]
        return remote(ref, ref, send.at[k], recv.at[k], device)

    begin = [
        go(0, y, c, None, dict(y=up)),
        go(1, y, c, None, dict(y=dn)),
        go(2, y, c, None, dict(c=oc)),
    ]
    for step in begin:
        step.start()
    begin[0].wait_recv()
    later = [go(3, dn, c, 0, dict(y=up)), go(4, dn, c, None, dict(c=oc))]
    for step in later:
        step.start()
    begin[1].wait_recv()
    later += [go(5, up, c, 1, dict(y=dn)), go(6, up, c, None, dict(c=oc))]
    for step in later[2:]:
        step.start()
    later[0].wait_recv()
    last = [go(7, op, c, 0, dict(c=oc)), go(8, op, c, 1, dict(c=oc))]
    last[0].start()
    later[2].wait_recv()
    last[1].start()
    begin[2].wait_recv()
    later[1].wait_recv()
    later[3].wait_recv()
    last[0].wait_recv()
    last[1].wait_recv()
    for step in begin + later + last:
        step.wait_send()


def embed_kernel(rows, first_out, normed_out, stage, far, near, other, total, rsend, rrecv, asend, arecv):
    me, y, c, up, dn, op, oc = ring_places()
    partner = dict(xl=1 - me["xl"], xh=1 - me["xh"])
    for device in (dict(y=up), dict(y=dn), dict(c=oc), partner):
        signal(device)
    pl.semaphore_wait(pltpu.get_barrier_semaphore(), 4)
    done = [
        to_owner(
            lambda b, role=role: rows.at[role, b],
            stage.at[role],
            far.at[role],
            near.at[role],
            rsend.at[role],
            rrecv.at[role],
        )
        for role in (1, 0)
    ]
    total[...] = done[0]().astype(BF16)
    cross = remote(total, other, rsend.at[2, 0], rrecv.at[2, 0], partner)
    cross.start()
    mine = done[1]()
    cross.wait()
    first = mine + other[...].astype(F32)
    first_out[...] = first.astype(BF16)
    normed_out[y, c] = normalize(first).astype(BF16)
    to_all(normed_out, asend, arecv)


def embed(rows):
    return pl.pallas_call(
        embed_kernel,
        out_shape=[
            jax.ShapeDtypeStruct((128, 1024), BF16),
            jax.ShapeDtypeStruct((4, 2, 128, 1024), BF16),
        ],
        in_specs=[VM],
        out_specs=[VM, VM],
        scratch_shapes=[
            pltpu.VMEM((2, 2, 128, 1024), BF16),
            pltpu.VMEM((2, 2, 64, 1024), BF16),
            pltpu.VMEM((2, 2, 128, 1024), BF16),
            pltpu.VMEM((128, 1024), BF16),
            pltpu.VMEM((128, 1024), BF16),
            pltpu.SemaphoreType.DMA((3, 4)),
            pltpu.SemaphoreType.DMA((3, 4)),
            pltpu.SemaphoreType.DMA((9,)),
            pltpu.SemaphoreType.DMA((9,)),
        ],
        compiler_params=params(4),
        name="embed_exchange",
    )(rows)


def pair_sum_to_owner(terms, pair, summed, stage, far, near, psend, precv, rsend, rrecv):
    me, y, c, up, dn, op, oc = ring_places()
    order = (op, up, dn, y)
    for device in (dict(y=up), dict(y=dn), dict(c=oc)):
        signal(device)
    pl.semaphore_wait(pltpu.get_barrier_semaphore(), 3)
    steps = [
        remote(terms.at[b, oc], pair.at[b], psend.at[i], precv.at[i], dict(c=oc))
        for i, b in enumerate(order)
    ]
    for step in steps:
        step.start()
    for i, b in enumerate(order):
        steps[i].wait_recv()
        summed[b] = (terms[b, c].astype(F32) + pair[b].astype(F32)).astype(BF16)
    total = to_owner(lambda b: summed.at[b], stage, far, near, rsend, rrecv)()
    for step in steps:
        step.wait_send()
    return total


PAIR_SCRATCH = [
    pltpu.VMEM((4, 128, 1024), BF16),
    pltpu.VMEM((4, 128, 1024), BF16),
    pltpu.VMEM((2, 128, 1024), BF16),
    pltpu.VMEM((2, 64, 1024), BF16),
    pltpu.VMEM((2, 128, 1024), BF16),
    pltpu.SemaphoreType.DMA((4,)),
    pltpu.SemaphoreType.DMA((4,)),
    pltpu.SemaphoreType.DMA((4,)),
    pltpu.SemaphoreType.DMA((4,)),
    pltpu.SemaphoreType.DMA((9,)),
    pltpu.SemaphoreType.DMA((9,)),
]


def residual_kernel(terms, first, second_out, normed_out, *scratch):
    me, y, c, up, dn, op, oc = ring_places()
    attn = pair_sum_to_owner(terms, *scratch[:9])
    second = (first[...].astype(F32) + attn).astype(BF16)
    second_out[...] = second
    normed_out[y, c] = normalize(second.astype(F32)).astype(BF16)
    to_all(normed_out, *scratch[9:])


def residual(terms, first):
    return pl.pallas_call(
        residual_kernel,
        out_shape=[
            jax.ShapeDtypeStruct((128, 1024), BF16),
            jax.ShapeDtypeStruct((4, 2, 128, 1024), BF16),
        ],
        in_specs=[VM, VM],
        out_specs=[VM, VM],
        scratch_shapes=PAIR_SCRATCH,
        compiler_params=params(5),
        name="residual_exchange",
    )(terms, first)


def backward_kernel(terms, second, g_third, g_out, *scratch):
    me, y, c, up, dn, op, oc = ring_places()
    grad = pair_sum_to_owner(terms, *scratch[:9])
    g_out[y, c] = (g_third[...] + normalize_back(second[...].astype(F32), grad)).astype(BF16)
    to_all(g_out, *scratch[9:])


def backward(terms, second, g_third):
    return pl.pallas_call(
        backward_kernel,
        out_shape=jax.ShapeDtypeStruct((4, 2, 128, 1024), BF16),
        in_specs=[VM, VM, VM],
        out_specs=VM,
        scratch_shapes=PAIR_SCRATCH,
        compiler_params=params(6),
        name="backward_exchange",
    )(terms, second, g_third)


PACKET = 512 + 1024 + 1024 + 128 + 128


def head_kernel(
    length, label, hidden_sum, second_sum, down_t, head, per_token_out, pulled_out, packet_out, parts, send, recv
):
    me, y, c, up, dn, op, oc = ring_places()
    slot = y * 2 + c
    peers = [(k, e) for k in (0, 1, 3, 2) for e in range(2) if (k, e) != (0, 0)]

    def device(k, e):
        return dict(y=add_mod(y, k, 4), c=add_mod(c, e, 2))

    for k, e in peers:
        signal(device(4 - k if k else 0, e))
    pl.semaphore_wait(pltpu.get_barrier_semaphore(), 7)
    contract = (((1,), (1,)), ((), ()))
    parts[slot] = second_sum[...] + lax.dot_general(
        hidden_sum[...], down_t[...].astype(F32), contract, precision=HIGH, preferred_element_type=F32
    )
    steps = [
        remote(parts.at[slot], parts.at[slot], send.at[k, e], recv.at[k, e], device(k, e)) for k, e in peers
    ]
    for step in steps:
        step.start()
    for step in steps:
        step.wait()
    pooled = parts[0]
    for s in range(1, 8):
        pooled = pooled + parts[s]
    count = length[0].astype(F32)
    pooled = pooled / count
    final = normalize(pooled)
    wide = head[...].astype(F32)
    logits = jnp.dot(final, wide, precision=HIGH, preferred_element_type=F32)
    top = jnp.max(logits, axis=-1, keepdims=True)
    total = jnp.log(jnp.sum(jnp.exp(logits - top), axis=-1, keepdims=True)) + top
    labels = (lax.broadcasted_iota(jnp.int32, logits.shape, 1) == label[0]).astype(F32)
    loss = total - jnp.sum(logits * labels, axis=-1, keepdims=True)
    g_logits = (jnp.exp(logits - total) - labels) / 16.0
    g_final = lax.dot_general(g_logits, wide, contract, precision=HIGH, preferred_element_type=F32)
    per_token = normalize_back(pooled, g_final) / count
    rounded = per_token.astype(BF16)
    per_token_out[...] = per_token
    pulled_out[...] = jnp.dot(rounded, down_t[...], preferred_element_type=F32)
    packet_out[:, 0:512] = hidden_sum[...]
    packet_out[:, 512:1536] = rounded.astype(F32)
    packet_out[:, 1536:2560] = final
    packet_out[:, 2560:2688] = g_logits
    packet_out[:, 2688:2816] = jnp.broadcast_to(loss, (1, 128))


def classify(length, label, hidden_sum, second_sum, down_t, head):
    return pl.pallas_call(
        head_kernel,
        out_shape=[
            jax.ShapeDtypeStruct((1, 1024), F32),
            jax.ShapeDtypeStruct((1, 512), F32),
            jax.ShapeDtypeStruct((1, PACKET), F32),
        ],
        in_specs=[SM, SM, VM, VM, VM, VM],
        out_specs=[VM, VM, VM],
        scratch_shapes=[
            pltpu.VMEM((8, 1, 1024), F32),
            pltpu.SemaphoreType.DMA((4, 2)),
            pltpu.SemaphoreType.DMA((4, 2)),
        ],
        compiler_params=params(7),
        name="classify",
    )(length, label, hidden_sum, second_sum, down_t, head)


SCALE = 0.125
WIDE = 256


def head_rows(value, head):
    rows = lax.broadcasted_iota(jnp.int32, value.shape, 0)
    return jnp.where((rows >= 64) == (head == 1), value, jnp.zeros_like(value))


def head_cols(value, head):
    cols = lax.broadcasted_iota(jnp.int32, value.shape, 1)
    return jnp.where((cols >= 64) == (head == 1), value, jnp.zeros_like(value))


def attend_kernel(length, qkv, context, context_t, probs_t):
    keys = qkv[:, 128:256]
    query_t = qkv[:, 0:128].T
    values_t = qkv[:, 256:384].T
    seen = lax.broadcasted_iota(jnp.int32, (1024, WIDE), 0) < length[0]
    for block in range(1024 // WIDE):
        cols = slice(block * WIDE, (block + 1) * WIDE)
        for head in range(2):
            scores = jnp.dot(keys, head_rows(query_t[:, cols], head), preferred_element_type=F32) * SCALE
            scores = jnp.where(seen, scores, -1e30)
            expo = jnp.exp(scores - jnp.max(scores, axis=0, keepdims=True))
            probs = (expo * (1.0 / jnp.sum(expo, axis=0, keepdims=True))).astype(BF16)
            probs_t[head, :, cols] = probs
            rows = slice(head * 64, head * 64 + 64)
            context_t[rows, cols] = jnp.dot(values_t[rows], probs, preferred_element_type=F32).astype(BF16)
    context[...] = context_t[...].T


def attend(length, qkv):
    return pl.pallas_call(
        attend_kernel,
        out_shape=[
            jax.ShapeDtypeStruct((1024, 128), BF16),
            jax.ShapeDtypeStruct((128, 1024), BF16),
            jax.ShapeDtypeStruct((2, 1024, 1024), BF16),
        ],
        in_specs=[SM, VM],
        out_specs=[VM, VM, VM],
        compiler_params=pltpu.CompilerParams(vmem_limit_bytes=48 * 2**20),
        name="attend",
    )(length, qkv)


def attend_back_kernel(qkv, probs_t, context_t, grad, out, grad_q, grad_k, grad_v):
    query = qkv[:, 0:128]
    keys_t = qkv[:, 128:256].T
    values = qkv[:, 256:384]
    grad_t = grad[...].T
    product = grad_t * context_t[...].astype(F32)
    for block in range(1024 // WIDE):
        cols = slice(block * WIDE, (block + 1) * WIDE)
        for head in range(2):
            rows = slice(head * 64, head * 64 + 64)
            probs = probs_t[head, :, cols]
            delta = jnp.sum(product[rows, cols], axis=0, keepdims=True)
            pulled = jnp.dot(values, head_rows(grad_t[:, cols], head).astype(BF16), preferred_element_type=F32)
            g_scores = (probs.astype(F32) * (pulled - delta) * SCALE).astype(BF16)
            grad_q[rows, cols] = jnp.dot(keys_t[rows], g_scores, preferred_element_type=F32)
            g_keys = jnp.dot(g_scores, head_cols(query[cols], head), preferred_element_type=F32)
            g_vals = jnp.dot(probs, head_cols(grad[cols], head).astype(BF16), preferred_element_type=F32)
            if block == 0 and head == 0:
                grad_k[...] = g_keys
                grad_v[...] = g_vals
            else:
                grad_k[...] += g_keys
                grad_v[...] += g_vals
    out[:, 0:128] = grad_q[...].T.astype(BF16)
    out[:, 128:256] = grad_k[...].astype(BF16)
    out[:, 256:384] = grad_v[...].astype(BF16)


def attend_back(qkv, probs_t, context_t, grad):
    return pl.pallas_call(
        attend_back_kernel,
        out_shape=jax.ShapeDtypeStruct((1024, 384), BF16),
        in_specs=[VM, VM, VM, VM],
        out_specs=VM,
        scratch_shapes=[
            pltpu.VMEM((128, 1024), F32),
            pltpu.VMEM((1024, 128), F32),
            pltpu.VMEM((1024, 128), F32),
        ],
        compiler_params=pltpu.CompilerParams(vmem_limit_bytes=48 * 2**20),
        name="attend_back",
    )(qkv, probs_t, context_t, grad)


def gelu(values):
    inner = jnp.tanh(0.7978845608028654 * (values + 0.044715 * values * values * values))
    return 0.5 * values * (1.0 + inner)


def gelu_slope(values):
    inner = jnp.tanh(0.7978845608028654 * (values + 0.044715 * values * values * values))
    return 0.5 * (1.0 + inner) + 0.5 * values * (1.0 - inner * inner) * 0.7978845608028654 * (
        1.0 + 3.0 * 0.044715 * values * values
    )


def per_device(token_ids, lengths, teacher_bins, table, qkv_shard, out_shard, up_shard, down_shard, head_shard):
    me = where_am_i()
    spot = (me["xl"] * 4 + me["z"]) * 2 + me["c"]
    vocab = table.shape[0]

    packet = jnp.concatenate(
        [
            token_ids,
            jnp.broadcast_to(lengths[:, None], (1, 128)),
            jnp.broadcast_to(teacher_bins[:, None], (1, 128)),
            jnp.zeros((5, 128), jnp.int32),
        ],
        axis=0,
    )
    got = spread_ids(packet)
    length = got[0, 0, 1, 0:1]
    label = got[0, 0, 2, 0:1]
    qkv_w, out_w, up_w, down_w, head_w = spread(
        [qkv_shard.reshape(64, 384), out_shard.T, up_shard, down_shard.T, head_shard]
    )
    qkv_w = qkv_w.reshape(1024, 384)
    out_w = out_w.reshape(1024, 128)
    up_w = up_w.reshape(1024, 512)
    down_w = down_w.reshape(1024, 512)
    head_w = head_w.reshape(1024, 128)

    shifted = got[:, :, 0, :] - (me["y"] * 2 + me["xh"]) * vocab
    inside = (shifted >= 0) & (shifted < vocab)
    rows = jnp.take(table, jnp.clip(shifted, 0, vocab - 1), axis=0)
    rows = jnp.where(inside[..., None], rows, jnp.zeros_like(rows))
    first, normed = embed(rows)
    normed = normed.reshape(1024, 1024)
    qkv = jnp.dot(normed, qkv_w, preferred_element_type=F32).astype(BF16)
    context, context_t, probs_t = attend(length, qkv)
    terms = jnp.einsum("ph,dh->pd", context, out_w, preferred_element_type=F32).astype(BF16)
    second, normed_two = residual(terms.reshape(4, 2, 128, 1024), first)
    normed_two = normed_two.reshape(1024, 1024)
    hidden = jnp.dot(normed_two, up_w, preferred_element_type=F32)
    live = (jnp.arange(1024, dtype=jnp.int32)[:, None] < length[0]).astype(F32)
    own = (me["y"] * 2 + me["c"]) * 128 + jnp.arange(128, dtype=jnp.int32)[:, None]
    live_own = (own < length[0]).astype(F32)
    hidden_sum = jnp.sum(gelu(hidden).astype(BF16).astype(F32) * live, axis=0, keepdims=True)
    second_sum = jnp.sum(second.astype(F32) * live_own, axis=0, keepdims=True)
    per_token, pulled, packet = classify(length, label, hidden_sum, second_sum, down_w, head_w)
    g_pre = (gelu_slope(hidden) * (pulled * live)).astype(BF16)
    up_term = jnp.einsum("pd,pf->df", normed_two, g_pre, preferred_element_type=F32).astype(BF16)
    terms = jnp.einsum("pf,df->pd", g_pre, up_w, preferred_element_type=F32).astype(BF16)
    g_second = backward(terms.reshape(4, 2, 128, 1024), second, per_token * live_own).reshape(1024, 1024)
    out_term = jnp.einsum("pd,ph->dh", g_second, context, preferred_element_type=F32).astype(BF16)
    g_context = jnp.einsum("pd,dh->ph", g_second, out_w, preferred_element_type=F32)
    g_qkv = attend_back(qkv, probs_t, context_t, g_context)
    qkv_term = jnp.einsum("pd,pr->dr", normed, g_qkv, preferred_element_type=F32).astype(BF16)
    packets, up_grad, out_grad, qkv_grad = collect(
        packet,
        [up_term.reshape(16, 64, 512), out_term.reshape(16, 64, 128), qkv_term.reshape(16, 64, 384)],
    )
    packets = packets.reshape(16, PACKET)
    loss = jnp.sum(packets[:, 2688]) / 16.0
    part = lax.dynamic_slice_in_dim(packets[:, 512:1536], spot * 64, 64, axis=1)
    down_grad = jnp.einsum("sf,sd->fd", packets[:, 0:512], part, precision=HIGH)
    part = lax.dynamic_slice_in_dim(packets[:, 1536:2560], spot * 64, 64, axis=1)
    head_grad = jnp.einsum("sd,sn->dn", part, packets[:, 2560:2688], precision=HIGH)
    return loss, qkv_grad.reshape(64, 3, 128), out_grad.T, up_grad, down_grad, head_grad


def solution(mesh):
    fine = Mesh(mesh.devices.reshape(2, 4, 2, 4, 2), ("xl", "z", "c", "y", "xh"))
    dp, tensor = ("xl", "z", "c"), ("y", "xh")
    return jax.shard_map(
        per_device,
        mesh=fine,
        in_specs=(
            P(dp, tensor),
            P(dp),
            P(dp),
            P(tensor, None),
            P(dp, None, tensor),
            P(tensor, dp),
            P(dp, tensor),
            P(tensor, dp),
            P(dp, None),
        ),
        out_specs=(
            P(),
            P(dp, None, tensor),
            P(tensor, dp),
            P(dp, tensor),
            P(tensor, dp),
            P(dp, None),
        ),
        check_vma=False,
    )
```

profile of v0, /device:TPU:1, one launch (start us, length us, event | category | flops | bytes accessed | tf_op | source)
XLA Modules:
  0.0 291.9 jit_solution(5090287183035565375)
XLA Ops:
  2.2 1.3 add_add_fusion.src
  3.5 10.9 %spread_ids.1 = s32[2,4,8,128]{3,2,1,0:T(8,128)} custom-call(s32[8,128]{1,0:T(8,128)} %add_add_fusion.src), custom_call_target="tpu_custom_call" | custom-call | tf_op jit(solution)/shard_map/spread_ids/pallas_call | solution.py:114
  19.3 9.2 %gather_fusion = bf16[1024,1024]{1,0:T(8,128)(2,1)S(1)} fusion(bf16[3816,1024]{1,0:T(8,128)(2,1)} %param.12, s32[1024]{0:T(1024)S(1)} %broadcast_clamp_fusion), kind=kCustom, calls=%fused_computation | custom fusion | bytes 4198400 | tf_op jit(solution)/shard_map/jit(_take)/gather | solution.py:667
  28.5 1.6 select_select_fusion.rows
  30.0 38.9 %embed_exchange.1 = (bf16[128,1024]{1,0:T(8,128)(2,1)}, bf16[4,2,128,1024]{3,2,1,0:T(8,128)(2,1)}) custom-call(bf16[2,4,128,1024]{3,2,1,0:T(8,128)(2,1)} %select_select_fusion.rows), custom_call_target="tpu_custom_call" | custom-call | tf_op jit(solution)/shard_map/embed_exchange/pallas_call | solution.py:361
  69.0 50.5 %spread_weights.1 = (bf16[16,64,384]{2,1,0:T(8,128)(2,1)}, bf16[16,64,128]{2,1,0:T(8,128)(2,1)}, bf16[16,64,512]{2,1,0:T(8,128)(2,1)}, bf16[16,64,512]{2,1,0:T(8,128)(2,1)}, bf16[16,64,128]{2,1,0:T(8,128)(2,1)}) custom-call(bf16[64,384]{1,0:T(8,128)(2,1)} %copy_bitcast_fusion.2.refs_0_, bf16[64,128]{1,0:T(8,128)(2,1)} %bitcast.81, bf16[64,512]{1,0:T(8,128)(2,1)} %refs_2_.1, ...), custom_call_target="tpu_custom_call" | custom-call | tf_op jit(solution)/shard_map/spread_weights/pallas_call | solution.py:213
  119.5 3.0 %convolution_convert_fusion.4.qkv = bf16[1024,384]{1,0:T(8,128)(2,1)S(1)} fusion(bf16[1024,1024]{1,0:T(8,128)(2,1)} %bitcast.85, bf16[1024,384]{1,0:T(8,128)(2,1)} %bitcast.91), kind=kOutput, calls=%fused_computation.17 | convolution fusion | flops 805699584 | bytes 3670016 | tf_op jit(solution)/shard_map/dot_general | solution.py:671
  122.5 7.9 %attend.1 = (bf16[1024,128]{1,0:T(8,128)(2,1)S(1)}, bf16[128,1024]{1,0:T(8,128)(2,1)S(1)}, bf16[2,1024,1024]{2,1,0:T(8,128)(2,1)S(1)}) custom-call(s32[1]{0:T(128)} %bitcast.2.length, bf16[1024,384]{1,0:T(8,128)(2,1)S(1)} %convolution_convert_fusion.4.qkv), custom_call_target="tpu_custom_call" | custom-call | tf_op jit(solution)/shard_map/attend/pallas_call | solution.py:569
  130.4 1.9 copy-done.1
  132.4 2.1 convolution_convert_fusion.1
  134.4 32.8 %residual_exchange.1 = (bf16[128,1024]{1,0:T(8,128)(2,1)}, bf16[4,2,128,1024]{3,2,1,0:T(8,128)(2,1)}) custom-call(bf16[4,2,128,1024]{3,2,1,0:T(8,128)(2,1)} %bitcast.61, bf16[128,1024]{1,0:T(8,128)(2,1)} %get-tuple-element.29.first), custom_call_target="tpu_custom_call" | custom-call | tf_op jit(solution)/shard_map/residual_exchange/pallas_call | solution.py:431
  167.2 1.7 multiply_reduce_fusion.1
  168.9 5.2 %multiply_reduce_fusion = (f32[512]{0:T(512)}, f32[1024,512]{1,0:T(8,128)}) fusion(f32[1024]{0:T(1024)S(1)} %fusion.13, bf16[1024,1024]{1,0:T(8,128)(2,1)} %bitcast.87, bf16[1024,512]{1,0:T(8,128)(2,1)S(1)} %bitcast.89), kind=kOutput, calls=%fused_computation.10 | convolution fusion | flops 1080032768 | bytes 5249024 | tf_op jit(solution)/shard_map/dot_general | solution.py:676
  174.1 14.4 %classify.1 = (f32[1,1024]{1,0:T(1,128)}, f32[1,512]{1,0:T(1,128)}, f32[1,2816]{1,0:T(1,128)}) custom-call(s32[1]{0:T(128)} %bitcast.2.length, s32[1]{0:T(128)} %bitcast.3.label, f32[1,512]{1,0:T(1,128)} %bitcast.84, f32[1,1024]{1,0:T(1,128)} %bitcast.79, bf16[1024,512]{1,0:T(8,128)(2,1)} %bitcast.66, bf16[1024,128]{1,0:T(8,128)(2,1)} %bitcast.74), custom_call_target="tpu_custom_call" | custom-call | tf_op jit(solution)/shard_map/classify/pallas_call | solution.py:517
  188.5 5.5 %convolution_convert_fusion.2 = bf16[1024,512]{1,0:T(8,128)(2,1)} fusion(bf16[1024,1024]{1,0:T(8,128)(2,1)} %bitcast.88, f32[1024,512]{1,0:T(8,128)} %get-tuple-element.61, f32[512]{0:T(512)} %bitcast.92, f32[1024]{0:T(1024)S(1)} %fusion.13), kind=kOutput, calls=%fused_computation.15 | convolution fusion | flops 1084751872 | bytes 5249024 | tf_op jit(solution)/shard_map/pd,pf->df/dot_general | solution.py:684
  194.1 3.6 %convolution_convert_fusion = bf16[1024,1024]{1,0:T(8,128)(2,1)} fusion(bf16[1024,512]{1,0:T(8,128)(2,1)S(1)} %bitcast.90, f32[1024,512]{1,0:T(8,128)S(1)} %copy-done.8, f32[512]{0:T(512)S(1)} %bitcast.93, f32[1024]{0:T(1024)S(1)} %fusion.13), kind=kOutput, calls=%fused_computation.13 | convolution fusion | flops 1085276160 | bytes 5249024 | tf_op jit(solution)/shard_map/pf,df->pd/dot_general | solution.py:685
  198.6 34.6 %backward_exchange.1 = bf16[4,2,128,1024]{3,2,1,0:T(8,128)(2,1)} custom-call(bf16[4,2,128,1024]{3,2,1,0:T(8,128)(2,1)} %bitcast.63, bf16[128,1024]{1,0:T(8,128)(2,1)} %get-tuple-element.32.second, f32[128,1024]{1,0:T(8,128)} %broadcast_multiply_fusion.g_third), custom_call_target="tpu_custom_call" | custom-call | tf_op jit(solution)/shard_map/backward_exchange/pallas_call | solution.py:453
  233.1 3.2 %convolution_convert_fusion.5 = bf16[1024,128]{1,0:T(8,128)(2,1)} fusion(bf16[1024,1024]{1,0:T(8,128)(2,1)} %bitcast.59, bf16[1024,128]{1,0:T(8,128)(2,1)S(1)} %get-tuple-element.27), kind=kOutput, calls=%fused_computation.18 | convolution fusion | flops 268566528 | bytes 2621440 | tf_op jit(solution)/shard_map/pd,ph->dh/dot_general | solution.py:687
  237.1 8.3 %attend_back.1 = bf16[1024,384]{1,0:T(8,128)(2,1)S(1)} custom-call(bf16[1024,384]{1,0:T(8,128)(2,1)S(1)} %convolution_convert_fusion.4.qkv, bf16[2,1024,1024]{2,1,0:T(8,128)(2,1)} %copy-done.1, bf16[128,1024]{1,0:T(8,128)(2,1)S(1)} %get-tuple-element.39.context_t, f32[1024,128]{1,0:T(8,128)S(1)} %fusion.20.grad), custom_call_target="tpu_custom_call" | custom-call | tf_op jit(solution)/shard_map/attend_back/pallas_call | solution.py:612
  245.4 2.2 convolution_convert_fusion.3
  247.6 34.5 %collect_gradients.1 = (f32[16,1,2816]{2,1,0:T(1,128)}, f32[64,512]{1,0:T(8,128)}, f32[64,128]{1,0:T(8,128)}, f32[64,384]{1,0:T(8,128)}) custom-call(f32[1,2816]{1,0:T(1,128)} %get-tuple-element.35.refs_0_, bf16[16,64,512]{2,1,0:T(8,128)(2,1)} %bitcast.65, bf16[16,64,128]{2,1,0:T(8,128)(2,1)} %bitcast.64, bf16[16,64,384]{2,1,0:T(8,128)(2,1)} %bitcast.69), custom_call_target="tpu_custom_call" | custom-call | tf_op jit(solution)/shard_map/collect_gradients/pallas_call | solution.py:242
  284.3 1.5 copy_bitcast_fusion.1
  287.8 1.4 copy.33
  289.2 1.6 copy.34
  (38 shorter events, 10.1 us)
Async XLA Ops:
  0.6 18.0 %copy-start = (bf16[64,3,128]{2,0,1:T(8,128)(2,1)S(1)}, bf16[64,3,128]{2,0,1:T(8,128)(2,1)}, u32[]{:S(2)}) copy-start(bf16[64,3,128]{2,0,1:T(8,128)(2,1)} %param.13) | copy-start | bytes 147460
  119.4 12.9 %copy-start.3 = (bf16[16,64,128]{2,1,0:T(8,128)(2,1)S(1)}, bf16[16,64,128]{2,1,0:T(8,128)(2,1)}, u32[]{:S(2)}) copy-start(bf16[16,64,128]{2,1,0:T(8,128)(2,1)} %get-tuple-element.28) | copy-start | bytes 786436
  130.4 1.9 copy-start.1
  132.4 36.5 %copy-start.6 = (bf16[16,64,512]{2,1,0:T(8,128)(2,1)S(1)}, bf16[16,64,512]{2,1,0:T(8,128)(2,1)}, u32[]{:S(2)}) copy-start(bf16[16,64,512]{2,1,0:T(8,128)(2,1)} %get-tuple-element.31) | copy-start | bytes 3145732
  188.5 5.6 %copy-start.7 = (f32[1,512]{1,0:T(1,128)S(1)}, f32[1,512]{1,0:T(1,128)}, u32[]{:S(2)}) copy-start(f32[1,512]{1,0:T(1,128)} %get-tuple-element.36) | copy-start | bytes 6148
  188.5 5.6 %copy-start.8 = (f32[1024,512]{1,0:T(8,128)S(1)}, f32[1024,512]{1,0:T(8,128)}, u32[]{:S(2)}) copy-start(f32[1024,512]{1,0:T(8,128)} %get-tuple-element.61) | copy-start | bytes 6291460
  194.1 3.6 %copy-start.4 = (f32[1,1024]{1,0:T(1,128)S(1)}, f32[1,1024]{1,0:T(1,128)}, u32[]{:S(2)}) copy-start(f32[1,1024]{1,0:T(1,128)} %get-tuple-element.37) | copy-start | bytes 12292
  233.1 3.2 %copy-start.2 = (bf16[4,2,128,1024]{3,2,1,0:T(8,128)(2,1)S(1)}, bf16[4,2,128,1024]{3,2,1,0:T(8,128)(2,1)}, u32[]{:S(2)}) copy-start(bf16[4,2,128,1024]{3,2,1,0:T(8,128)(2,1)} %backward_exchange.1) | copy-start | bytes 6291460
  237.1 8.3 %copy-start.5 = (bf16[4,2,128,1024]{3,2,1,0:T(8,128)(2,1)S(1)}, bf16[4,2,128,1024]{3,2,1,0:T(8,128)(2,1)}, u32[]{:S(2)}) copy-start(bf16[4,2,128,1024]{3,2,1,0:T(8,128)(2,1)} %get-tuple-element.25) | copy-start | bytes 6291460
where the time goes:
time: 293 us; the launch traced here: 292 us
  Pallas kernels  233 us (80%)
  matrix products  27.5 us (9%)
  local copies, waits for them, and re-layouts  18.7 us (6%)
  other arithmetic  8.91 us (3%)
  between operations  3.96 us (1%)
    pallas_call x1, Pallas kernels, spread(): pl.pallas_call(functools.partial(spread_kernel, count), out_shape=[jax.Sh...  50.5 us
    pallas_call x1, Pallas kernels, embed(): pl.pallas_call(embed_kernel, out_shape=[jax.ShapeDtypeStruct((128, 1024),...  38.9 us
    pallas_call x1, Pallas kernels, backward(): pl.pallas_call(backward_kernel, out_shape=jax.ShapeDtypeStruct((4, 2, 128...  34.6 us
    pallas_call x1, Pallas kernels, collect(): pl.pallas_call(functools.partial(collect_kernel, count), out_shape=shapes...  34.5 us
    pallas_call x1, Pallas kernels, residual(): pl.pallas_call(residual_kernel, out_shape=[jax.ShapeDtypeStruct((128, 102...  32.8 us
    pallas_call x1, Pallas kernels, classify(): pl.pallas_call(head_kernel, out_shape=[jax.ShapeDtypeStruct((1, 1024), F3...  14.4 us
    pallas_call x1, Pallas kernels, spread_ids(): pl.pallas_call(spread_ids_kernel, out_shape=jax.ShapeDtypeStruct((2, 4, 8...  10.9 us
    gather x1, local copies, waits for them, and re-layouts, per_device(): rows = jnp.take(table, jnp.clip(shifted, 0, vocab - 1), axis=0)  9.2 us

commit v1 on v0

--- a/solution.py
+++ b/solution.py
@@ -122,133 +122,156 @@
     )(packet)
 
 
-def plane_kernel(count, collect, *refs):
-    me = where_am_i()
-    xl, z, c, y, xh = (me[n] for n in ("xl", "z", "c", "y", "xh"))
-    here = xh == c
-    srcs, dsts = refs[:count], refs[count : 2 * count]
-    send, recv = refs[2 * count :]
-    mine, other = (xh, c) if collect else (c, xh)
-
-    def target(a, k, e):
-        swapped = dict(c=e, xh=c) if collect else dict(c=xh, xh=e)
-        return dict(xl=add_mod(xl, a, 2), z=add_mod(z, k, 4), y=y, **swapped)
-
-    def origin(a, k, e):
-        swapped = dict(c=xh, xh=e) if collect else dict(c=e, xh=c)
-        return dict(xl=add_mod(xl, a, 2), z=add_mod(z, 4 - k, 4), y=y, **swapped)
-
-    def number(a, k, e, back):
-        return (add_mod(xl, a, 2) * 4 + add_mod(z, 4 - k if back else k, 4)) * 2 + e
-
-    slot = (xl * 4 + z) * 2 + mine
-
-    def block(i, a, k, e):
-        if collect and len(srcs[i].shape) == 3 and srcs[i].shape[0] == 16:
-            return srcs[i].at[number(a, k, e, False)]
-        return srcs[i]
-
-    def copy(i, a, k, e):
+class Plane:
+    def __init__(self, srcs, dsts, send, recv, collect):
+        self.srcs, self.dsts, self.send, self.recv, self.collect = srcs, dsts, send, recv, collect
+        self.me = where_am_i()
+        c, xh = self.me["c"], self.me["xh"]
+        self.here = xh == c
+        self.mine, self.other = (xh, c) if collect else (c, xh)
+        self.slot = (self.me["xl"] * 4 + self.me["z"]) * 2 + self.mine
+        self.places = [(a, k, e) for k in (2, 1, 3, 0) for a in (1, 0) for e in range(2)]
+
+    def target(self, a, k, e):
+        me = self.me
+        swapped = dict(c=e, xh=me["c"]) if self.collect else dict(c=me["xh"], xh=e)
+        return dict(xl=add_mod(me["xl"], a, 2), z=add_mod(me["z"], k, 4), y=me["y"], **swapped)
+
+    def origin(self, a, k, e):
+        me = self.me
+        swapped = dict(c=me["xh"], xh=e) if self.collect else dict(c=e, xh=me["c"])
+        return dict(xl=add_mod(me["xl"], a, 2), z=add_mod(me["z"], 4 - k, 4), y=me["y"], **swapped)
+
+    def number(self, a, k, e, back):
+        me = self.me
+        return (add_mod(me["xl"], a, 2) * 4 + add_mod(me["z"], 4 - k if back else k, 4)) * 2 + e
+
+    def block(self, i, a, k, e):
+        if self.collect and len(self.srcs[i].shape) == 3 and self.srcs[i].shape[0] == 16:
+            return self.srcs[i].at[self.number(a, k, e, False)]
+        return self.srcs[i]
+
+    def copy(self, i, a, k, e):
         return remote(
-            block(i, a, k, e),
-            dsts[i].at[slot],
-            send.at[i, a, k, e],
-            recv.at[i, a, k, mine],
-            target(a, k, e),
+            self.block(i, a, k, e),
+            self.dsts[i].at[self.slot],
+            self.send.at[i, a, k, e],
+            self.recv.at[i, a, k, self.mine],
+            self.target(a, k, e),
         )
 
-    places = [(a, k, e) for k in (1, 3, 2, 0) for a in (1, 0) for e in range(2)]
-
-    def is_self(a, k, e):
-        return jnp.logical_and(here, e == other)
-
-    for a, k, e in places:
-        if a == 0 and k == 0:
-            @pl.when(jnp.logical_not(jnp.logical_and(here, e == mine)))
-            def _(a=a, k=k, e=e):
-                signal(origin(a, k, e))
-        else:
-            signal(origin(a, k, e))
-    pl.semaphore_wait(pltpu.get_barrier_semaphore(), jnp.where(here, 15, 16))
-    for i in range(count):
-        for a, k, e in places:
+    def greet(self):
+        for a, k, e in self.places:
             if a == 0 and k == 0:
 
-                @pl.when(jnp.logical_not(is_self(a, k, e)))
-                def _(i=i, a=a, k=k, e=e):
-                    copy(i, a, k, e).start()
-
-                @pl.when(is_self(a, k, e))
-                def _(i=i, a=a, k=k, e=e):
+                @pl.when(jnp.logical_not(jnp.logical_and(self.here, e == self.mine)))
+                def _(a=a, k=k, e=e):
+                    signal(self.origin(a, k, e))
+            else:
+                signal(self.origin(a, k, e))
+        return jnp.where(self.here, 15, 16)
+
+    def is_self(self, e):
+        return jnp.logical_and(self.here, e == self.other)
+
+    def start(self, i):
+        for a, k, e in self.places:
+            if a == 0 and k == 0:
+
+                @pl.when(jnp.logical_not(self.is_self(e)))
+                def _(a=a, k=k, e=e):
+                    self.copy(i, a, k, e).start()
+
+                @pl.when(self.is_self(e))
+                def _(a=a, k=k, e=e):
                     pltpu.make_async_copy(
-                        block(i, a, k, e), dsts[i].at[slot], recv.at[i, a, k, mine]
+                        self.block(i, a, k, e), self.dsts[i].at[self.slot], self.recv.at[i, a, k, self.mine]
                     ).start()
             else:
-                copy(i, a, k, e).start()
-
-    def finish(i):
-        for a, k, e in places:
+                self.copy(i, a, k, e).start()
+
+    def finish(self, i):
+        for a, k, e in self.places:
             if a == 0 and k == 0:
 
-                @pl.when(jnp.logical_not(is_self(a, k, e)))
+                @pl.when(jnp.logical_not(self.is_self(e)))
                 def _(a=a, k=k, e=e):
-                    copy(i, a, k, e).wait_send()
+                    self.copy(i, a, k, e).wait_send()
             else:
-                copy(i, a, k, e).wait_send()
+                self.copy(i, a, k, e).wait_send()
             pltpu.make_async_copy(
-                block(i, 0, 0, 0), dsts[i].at[number(a, k, e, True)], recv.at[i, a, k, e]
+                self.block(i, 0, 0, 0), self.dsts[i].at[self.number(a, k, e, True)], self.recv.at[i, a, k, e]
             ).wait()
 
-    return finish
-
-
-def spread_kernel(count, *refs):
-    finish = plane_kernel(count, False, *refs)
-    for i in range(count):
-        finish(i)
-
-
-def spread(shards):
-    count = len(shards)
+
+def plane_sems(count):
+    return [pltpu.SemaphoreType.DMA((count, 2, 4, 2))] * 2
+
+
+def gathered(shard):
+    return jax.ShapeDtypeStruct((16, *shard.shape), shard.dtype)
+
+
+def total_of(buf):
+    total = buf[0].astype(F32)
+    for s in range(1, 16):
+        total = total + buf[s].astype(F32)
+    return total
+
+
+def thirds(row):
+    high = row.astype(BF16).astype(F32)
+    middle = (row - high).astype(BF16).astype(F32)
+    low = row - high - middle
+    index = lax.broadcasted_iota(jnp.int32, (8, row.shape[1]), 0)
+    rows = jnp.where(index == 0, high, jnp.where(index == 1, middle, jnp.where(index == 2, low, 0.0)))
+    return rows.astype(BF16)
+
+
+def picked(values, start):
+    rows = lax.broadcasted_iota(jnp.int32, (values.shape[1], 64), 0)
+    cols = lax.broadcasted_iota(jnp.int32, (values.shape[1], 64), 1)
+    chosen = (rows == cols + start).astype(F32)
+    return jnp.dot(values, chosen, precision=HIGH, preferred_element_type=F32)
+
+
+def collect_kernel(packets, out_term, qkv_term, out_grad, qkv_grad, down_grad, head_grad, loss, out_buf, qkv_buf, send, recv):
+    plane = Plane([out_term, qkv_term], [out_buf, qkv_buf], send, recv, True)
+    pl.semaphore_wait(pltpu.get_barrier_semaphore(), plane.greet())
+    plane.start(0)
+    plane.start(1)
+    me = plane.me
+    start = ((me["xl"] * 4 + me["z"]) * 2 + me["c"]) * 64
+    over = (((0,), (0,)), ((), ()))
+    down_grad[...] = lax.dot_general(
+        packets[:, 0:512], picked(packets[:, 512:1536], start), over, precision=HIGH, preferred_element_type=F32
+    )
+    head_grad[...] = lax.dot_general(
+        picked(packets[:, 1536:2560], start), packets[:, 2560:2688], over, precision=HIGH, preferred_element_type=F32
+    )
+    loss[...] = jnp.sum(packets[:, 2688:2816], axis=0, keepdims=True) / 16.0
+    plane.finish(0)
+    out_grad[...] = total_of(out_buf)
+    plane.finish(1)
+    qkv_grad[...] = total_of(qkv_buf)
+
+
+def collect(packets, out_term, qkv_term):
     return pl.pallas_call(
-        functools.partial(spread_kernel, count),
-        out_shape=[jax.ShapeDtypeStruct((16, *s.shape), s.dtype) for s in shards],
-        in_specs=[VM] * count,
-        out_specs=[VM] * count,
-        scratch_shapes=[pltpu.SemaphoreType.DMA((count, 2, 4, 2))] * 2,
-        compiler_params=params(2),
-        name="spread_weights",
-    )(*shards)
-
-
-def collect_kernel(count, *refs):
-    ins, outs = refs[:count], refs[count : 2 * count]
-    bufs = refs[2 * count : 3 * count - 1]
-    sems = refs[3 * count - 1 :]
-    finish = plane_kernel(count, True, *ins, outs[0], *bufs, *sems)
-    finish(0)
-    for i in range(1, count):
-        finish(i)
-        total = bufs[i - 1][0].astype(F32)
-        for s in range(1, 16):
-            total = total + bufs[i - 1][s].astype(F32)
-        outs[i][...] = total
-
-
-def collect(packet, grads):
-    count = 1 + len(grads)
-    shapes = [jax.ShapeDtypeStruct((16, *packet.shape), packet.dtype)]
-    shapes += [jax.ShapeDtypeStruct(g.shape[1:], F32) for g in grads]
-    return pl.pallas_call(
-        functools.partial(collect_kernel, count),
-        out_shape=shapes,
-        in_specs=[VM] * count,
-        out_specs=[VM] * count,
-        scratch_shapes=[pltpu.VMEM(g.shape, g.dtype) for g in grads]
-        + [pltpu.SemaphoreType.DMA((count, 2, 4, 2))] * 2,
+        collect_kernel,
+        out_shape=[
+            jax.ShapeDtypeStruct((64, 128), F32),
+            jax.ShapeDtypeStruct((64, 384), F32),
+            jax.ShapeDtypeStruct((512, 64), F32),
+            jax.ShapeDtypeStruct((64, 128), F32),
+            jax.ShapeDtypeStruct((1, 128), F32),
+        ],
+        in_specs=[VM] * 3,
+        out_specs=[VM] * 5,
+        scratch_shapes=[pltpu.VMEM((16, 64, 128), BF16), pltpu.VMEM((16, 64, 384), BF16), *plane_sems(2)],
         compiler_params=params(3),
         name="collect_gradients",
-    )(packet, *grads)
+    )(packets, out_term, qkv_term)
 
 
 def ring_places():
@@ -260,7 +283,7 @@
 HALVES = (pl.ds(0, 64), pl.ds(64, 64))
 
 
-def to_owner(blocks, stage, far, near, send, recv):
+def to_owner(blocks, stage, far, near, send, recv, meanwhile=None):
     me, y, c, up, dn, op, oc = ring_places()
     first = [
         remote(blocks(op).at[HALVES[0]], far.at[0], send.at[0], recv.at[0], dict(y=up)),
@@ -268,6 +291,8 @@
     ]
     for step in first:
         step.start()
+    if meanwhile is not None:
+        meanwhile()
 
     def second(side):
         return remote(
@@ -329,12 +354,16 @@
         step.wait_send()
 
 
-def embed_kernel(rows, first_out, normed_out, stage, far, near, other, total, rsend, rrecv, asend, arecv):
+def embed_kernel(
+    rows, qkv_s, out_s, head_s, first_out, normed_out, qkv_w, out_w, head_w,
+    stage, far, near, other, total, rsend, rrecv, asend, arecv, psend, precv,
+):
     me, y, c, up, dn, op, oc = ring_places()
+    plane = Plane([qkv_s, out_s, head_s], [qkv_w, out_w, head_w], psend, precv, False)
     partner = dict(xl=1 - me["xl"], xh=1 - me["xh"])
     for device in (dict(y=up), dict(y=dn), dict(c=oc), partner):
         signal(device)
-    pl.semaphore_wait(pltpu.get_barrier_semaphore(), 4)
+    pl.semaphore_wait(pltpu.get_barrier_semaphore(), plane.greet() + 4)
     done = [
         to_owner(
             lambda b, role=role: rows.at[role, b],
@@ -343,6 +372,7 @@
             near.at[role],
             rsend.at[role],
             rrecv.at[role],
+            (lambda: [plane.start(i) for i in range(3)]) if role == 1 else None,
         )
         for role in (1, 0)
     ]
@@ -355,17 +385,20 @@
     first_out[...] = first.astype(BF16)
     normed_out[y, c] = normalize(first).astype(BF16)
     to_all(normed_out, asend, arecv)
-
-
-def embed(rows):
+    for i in range(3):
+        plane.finish(i)
+
+
+def embed(rows, shards):
     return pl.pallas_call(
         embed_kernel,
         out_shape=[
             jax.ShapeDtypeStruct((128, 1024), BF16),
             jax.ShapeDtypeStruct((4, 2, 128, 1024), BF16),
-        ],
-        in_specs=[VM],
-        out_specs=[VM, VM],
+            *map(gathered, shards),
+        ],
+        in_specs=[VM] * 4,
+        out_specs=[VM] * 5,
         scratch_shapes=[
             pltpu.VMEM((2, 2, 128, 1024), BF16),
             pltpu.VMEM((2, 2, 64, 1024), BF16),
@@ -376,24 +409,27 @@
             pltpu.SemaphoreType.DMA((3, 4)),
             pltpu.SemaphoreType.DMA((9,)),
             pltpu.SemaphoreType.DMA((9,)),
+            *plane_sems(3),
         ],
         compiler_params=params(4),
         name="embed_exchange",
-    )(rows)
-
-
-def pair_sum_to_owner(terms, pair, summed, stage, far, near, psend, precv, rsend, rrecv):
+    )(rows, *shards)
+
+
+def pair_sum_to_owner(plane, terms, pair, summed, stage, far, near, psend, precv, rsend, rrecv):
     me, y, c, up, dn, op, oc = ring_places()
     order = (op, up, dn, y)
     for device in (dict(y=up), dict(y=dn), dict(c=oc)):
         signal(device)
-    pl.semaphore_wait(pltpu.get_barrier_semaphore(), 3)
+    pl.semaphore_wait(pltpu.get_barrier_semaphore(), plane.greet() + 3)
     steps = [
         remote(terms.at[b, oc], pair.at[b], psend.at[i], precv.at[i], dict(c=oc))
         for i, b in enumerate(order)
     ]
     for step in steps:
         step.start()
+    for i in range(len(plane.srcs)):
+        plane.start(i)
     for i, b in enumerate(order):
         steps[i].wait_recv()
         summed[b] = (terms[b, c].astype(F32) + pair[b].astype(F32)).astype(BF16)
@@ -415,50 +451,63 @@
     pltpu.SemaphoreType.DMA((4,)),
     pltpu.SemaphoreType.DMA((9,)),
     pltpu.SemaphoreType.DMA((9,)),
+    *plane_sems(2),
 ]
 
 
-def residual_kernel(terms, first, second_out, normed_out, *scratch):
+def residual_kernel(terms, first, up_s, down_s, second_out, normed_out, up_w, down_w, *scratch):
     me, y, c, up, dn, op, oc = ring_places()
-    attn = pair_sum_to_owner(terms, *scratch[:9])
+    plane = Plane([up_s, down_s], [up_w, down_w], *scratch[11:], False)
+    attn = pair_sum_to_owner(plane, terms, *scratch[:9])
     second = (first[...].astype(F32) + attn).astype(BF16)
     second_out[...] = second
     normed_out[y, c] = normalize(second.astype(F32)).astype(BF16)
-    to_all(normed_out, *scratch[9:])
-
-
-def residual(terms, first):
+    to_all(normed_out, *scratch[9:11])
+    plane.finish(0)
+    plane.finish(1)
+
+
+def residual(terms, first, shards):
     return pl.pallas_call(
         residual_kernel,
         out_shape=[
             jax.ShapeDtypeStruct((128, 1024), BF16),
             jax.ShapeDtypeStruct((4, 2, 128, 1024), BF16),
-        ],
-        in_specs=[VM, VM],
-        out_specs=[VM, VM],
+            *map(gathered, shards),
+        ],
+        in_specs=[VM] * 4,
+        out_specs=[VM] * 4,
         scratch_shapes=PAIR_SCRATCH,
         compiler_params=params(5),
         name="residual_exchange",
-    )(terms, first)
-
-
-def backward_kernel(terms, second, g_third, g_out, *scratch):
+    )(terms, first, *shards)
+
+
+def backward_kernel(terms, second, g_third, up_term, packet, g_out, up_grad, packets, up_buf, *scratch):
     me, y, c, up, dn, op, oc = ring_places()
-    grad = pair_sum_to_owner(terms, *scratch[:9])
+    plane = Plane([packet, up_term], [packets, up_buf], *scratch[11:], True)
+    grad = pair_sum_to_owner(plane, terms, *scratch[:9])
     g_out[y, c] = (g_third[...] + normalize_back(second[...].astype(F32), grad)).astype(BF16)
-    to_all(g_out, *scratch[9:])
-
-
-def backward(terms, second, g_third):
+    to_all(g_out, *scratch[9:11])
+    plane.finish(0)
+    plane.finish(1)
+    up_grad[...] = total_of(up_buf)
+
+
+def backward(terms, second, g_third, up_term, packet):
     return pl.pallas_call(
         backward_kernel,
-        out_shape=jax.ShapeDtypeStruct((4, 2, 128, 1024), BF16),
-        in_specs=[VM, VM, VM],
-        out_specs=VM,
-        scratch_shapes=PAIR_SCRATCH,
+        out_shape=[
+            jax.ShapeDtypeStruct((4, 2, 128, 1024), BF16),
+            jax.ShapeDtypeStruct((64, 512), F32),
+            gathered(packet),
+        ],
+        in_specs=[VM] * 5,
+        out_specs=[VM] * 3,
+        scratch_shapes=[pltpu.VMEM((16, 64, 512), BF16), *PAIR_SCRATCH],
         compiler_params=params(6),
         name="backward_exchange",
-    )(terms, second, g_third)
+    )(terms, second, g_third, up_term, packet)
 
 
 PACKET = 512 + 1024 + 1024 + 128 + 128
@@ -478,9 +527,8 @@
         signal(device(4 - k if k else 0, e))
     pl.semaphore_wait(pltpu.get_barrier_semaphore(), 7)
     contract = (((1,), (1,)), ((), ()))
-    parts[slot] = second_sum[...] + lax.dot_general(
-        hidden_sum[...], down_t[...].astype(F32), contract, precision=HIGH, preferred_element_type=F32
-    )
+    pushed = lax.dot_general(thirds(hidden_sum[...]), down_t[...], contract, preferred_element_type=F32)
+    parts[slot] = second_sum[...] + jnp.sum(pushed, axis=0, keepdims=True)
     steps = [
         remote(parts.at[slot], parts.at[slot], send.at[k, e], recv.at[k, e], device(k, e)) for k, e in peers
     ]
@@ -494,14 +542,14 @@
     count = length[0].astype(F32)
     pooled = pooled / count
     final = normalize(pooled)
-    wide = head[...].astype(F32)
-    logits = jnp.dot(final, wide, precision=HIGH, preferred_element_type=F32)
+    logits = jnp.sum(jnp.dot(thirds(final), head[...], preferred_element_type=F32), axis=0, keepdims=True)
     top = jnp.max(logits, axis=-1, keepdims=True)
     total = jnp.log(jnp.sum(jnp.exp(logits - top), axis=-1, keepdims=True)) + top
     labels = (lax.broadcasted_iota(jnp.int32, logits.shape, 1) == label[0]).astype(F32)
     loss = total - jnp.sum(logits * labels, axis=-1, keepdims=True)
     g_logits = (jnp.exp(logits - total) - labels) / 16.0
-    g_final = lax.dot_general(g_logits, wide, contract, precision=HIGH, preferred_element_type=F32)
+    g_final = lax.dot_general(thirds(g_logits), head[...], contract, preferred_element_type=F32)
+    g_final = jnp.sum(g_final, axis=0, keepdims=True)
     per_token = normalize_back(pooled, g_final) / count
     rounded = per_token.astype(BF16)
     per_token_out[...] = per_token
@@ -638,7 +686,6 @@
 
 def per_device(token_ids, lengths, teacher_bins, table, qkv_shard, out_shard, up_shard, down_shard, head_shard):
     me = where_am_i()
-    spot = (me["xl"] * 4 + me["z"]) * 2 + me["c"]
     vocab = table.shape[0]
 
     packet = jnp.concatenate(
@@ -653,25 +700,21 @@
     got = spread_ids(packet)
     length = got[0, 0, 1, 0:1]
     label = got[0, 0, 2, 0:1]
-    qkv_w, out_w, up_w, down_w, head_w = spread(
-        [qkv_shard.reshape(64, 384), out_shard.T, up_shard, down_shard.T, head_shard]
-    )
-    qkv_w = qkv_w.reshape(1024, 384)
-    out_w = out_w.reshape(1024, 128)
-    up_w = up_w.reshape(1024, 512)
-    down_w = down_w.reshape(1024, 512)
-    head_w = head_w.reshape(1024, 128)
-
     shifted = got[:, :, 0, :] - (me["y"] * 2 + me["xh"]) * vocab
     inside = (shifted >= 0) & (shifted < vocab)
     rows = jnp.take(table, jnp.clip(shifted, 0, vocab - 1), axis=0)
     rows = jnp.where(inside[..., None], rows, jnp.zeros_like(rows))
-    first, normed = embed(rows)
+    first, normed, qkv_w, out_w, head_w = embed(rows, [qkv_shard.reshape(64, 384), out_shard.T, head_shard])
+    qkv_w = qkv_w.reshape(1024, 384)
+    out_w = out_w.reshape(1024, 128)
+    head_w = head_w.reshape(1024, 128)
     normed = normed.reshape(1024, 1024)
     qkv = jnp.dot(normed, qkv_w, preferred_element_type=F32).astype(BF16)
     context, context_t, probs_t = attend(length, qkv)
     terms = jnp.einsum("ph,dh->pd", context, out_w, preferred_element_type=F32).astype(BF16)
-    second, normed_two = residual(terms.reshape(4, 2, 128, 1024), first)
+    second, normed_two, up_w, down_w = residual(terms.reshape(4, 2, 128, 1024), first, [up_shard, down_shard.T])
+    up_w = up_w.reshape(1024, 512)
+    down_w = down_w.reshape(1024, 512)
     normed_two = normed_two.reshape(1024, 1024)
     hidden = jnp.dot(normed_two, up_w, preferred_element_type=F32)
     live = (jnp.arange(1024, dtype=jnp.int32)[:, None] < length[0]).astype(F32)
@@ -683,22 +726,18 @@
     g_pre = (gelu_slope(hidden) * (pulled * live)).astype(BF16)
     up_term = jnp.einsum("pd,pf->df", normed_two, g_pre, preferred_element_type=F32).astype(BF16)
     terms = jnp.einsum("pf,df->pd", g_pre, up_w, preferred_element_type=F32).astype(BF16)
-    g_second = backward(terms.reshape(4, 2, 128, 1024), second, per_token * live_own).reshape(1024, 1024)
+    g_second, up_grad, packets = backward(
+        terms.reshape(4, 2, 128, 1024), second, per_token * live_own, up_term.reshape(16, 64, 512), packet
+    )
+    g_second = g_second.reshape(1024, 1024)
     out_term = jnp.einsum("pd,ph->dh", g_second, context, preferred_element_type=F32).astype(BF16)
     g_context = jnp.einsum("pd,dh->ph", g_second, out_w, preferred_element_type=F32)
     g_qkv = attend_back(qkv, probs_t, context_t, g_context)
     qkv_term = jnp.einsum("pd,pr->dr", normed, g_qkv, preferred_element_type=F32).astype(BF16)
-    packets, up_grad, out_grad, qkv_grad = collect(
-        packet,
-        [up_term.reshape(16, 64, 512), out_term.reshape(16, 64, 128), qkv_term.reshape(16, 64, 384)],
-    )
-    packets = packets.reshape(16, PACKET)
-    loss = jnp.sum(packets[:, 2688]) / 16.0
-    part = lax.dynamic_slice_in_dim(packets[:, 512:1536], spot * 64, 64, axis=1)
-    down_grad = jnp.einsum("sf,sd->fd", packets[:, 0:512], part, precision=HIGH)
-    part = lax.dynamic_slice_in_dim(packets[:, 1536:2560], spot * 64, 64, axis=1)
-    head_grad = jnp.einsum("sd,sn->dn", part, packets[:, 2560:2688], precision=HIGH)
-    return loss, qkv_grad.reshape(64, 3, 128), out_grad.T, up_grad, down_grad, head_grad
+    out_grad, qkv_grad, down_grad, head_grad, loss = collect(
+        packets.reshape(16, PACKET), out_term.reshape(16, 64, 128), qkv_term.reshape(16, 64, 384)
+    )
+    return loss[0, 0], qkv_grad.reshape(64, 3, 128), out_grad.T, up_grad, down_grad, head_grad
 
 
 def solution(mesh):

time: 293 us -> 237 us (0.81)
  Pallas kernels: 233 us -> 178 us
    pallas_call x3 -> x2, Pallas kernels: 120 us -> 57.3 us  [the longest x1 36.5 us: backward(): pl.pallas_call(backward_kernel, out_shape=[jax.ShapeDtypeStruct((4, 2, 12...]
    pallas_call x1, Pallas kernels: 38.9 us -> 47.3 us  [embed(): pl.pallas_call(embed_kernel, out_shape=[jax.ShapeDtypeStruct((128, 1024),...]
    pallas_call x1, Pallas kernels: 14.4 us -> 11.1 us  [classify(): pl.pallas_call(head_kernel, out_shape=[jax.ShapeDtypeStruct((1, 1024), F3...]
    unnamed x23 -> x31, local copies, waits for them, and re-layouts: 7.4 us -> 9.34 us
where the time goes in v1:
time: 237 us; the launch traced here: 236 us
  Pallas kernels  178 us (75%)
  matrix products  25.8 us (11%)
  local copies, waits for them, and re-layouts  20.7 us (9%)
  other arithmetic  7.38 us (3%)
  between operations  3.99 us (2%)
    pallas_call x1, Pallas kernels, embed(): pl.pallas_call(embed_kernel, out_shape=[jax.ShapeDtypeStruct((128, 1024),...  47.3 us
    pallas_call x1, Pallas kernels, backward(): pl.pallas_call(backward_kernel, out_shape=[jax.ShapeDtypeStruct((4, 2, 12...  36.5 us
    pallas_call x1, Pallas kernels, residual(): pl.pallas_call(residual_kernel, out_shape=[jax.ShapeDtypeStruct((128, 102...  35.2 us
    pallas_call x1, Pallas kernels, collect(): pl.pallas_call(collect_kernel, out_shape=[jax.ShapeDtypeStruct((64, 128),...  20.9 us
    pallas_call x1, Pallas kernels, classify(): pl.pallas_call(head_kernel, out_shape=[jax.ShapeDtypeStruct((1, 1024), F3...  11.1 us
    pallas_call x1, Pallas kernels, spread_ids(): pl.pallas_call(spread_ids_kernel, out_shape=jax.ShapeDtypeStruct((2, 4, 8...  10.9 us
    unnamed x31, local copies, waits for them, and re-layouts  9.34 us
    gather x1, local copies, waits for them, and re-layouts, per_device(): rows = jnp.take(table, jnp.clip(shifted, 0, vocab - 1), axis=0)  9.2 us

profile of v1, /device:TPU:1, one launch (start us, length us, event | category | flops | bytes accessed | tf_op | source)
XLA Modules:
  0.0 235.8 jit_solution(11501145730779589945)
XLA Ops:
  2.2 1.3 add_add_fusion.src
  3.5 10.9 %spread_ids.1 = s32[2,4,8,128]{3,2,1,0:T(8,128)} custom-call(s32[8,128]{1,0:T(8,128)} %add_add_fusion.src), custom_call_target="tpu_custom_call" | custom-call | tf_op jit(solution)/shard_map/spread_ids/pallas_call | solution.py:114
  15.3 9.2 %gather_fusion = bf16[1024,1024]{1,0:T(8,128)(2,1)S(1)} fusion(bf16[3816,1024]{1,0:T(8,128)(2,1)} %param.12, s32[1024]{0:T(1024)S(1)} %broadcast_clamp_fusion), kind=kCustom, calls=%fused_computation | custom fusion | bytes 4198400 | tf_op jit(solution)/shard_map/jit(_take)/gather | solution.py:705
  25.3 1.6 select_select_fusion.rows
  27.5 47.3 %embed_exchange.1 = (bf16[128,1024]{1,0:T(8,128)(2,1)}, bf16[4,2,128,1024]{3,2,1,0:T(8,128)(2,1)}, bf16[16,64,384]{2,1,0:T(8,128)(2,1)}, bf16[16,64,128]{2,1,0:T(8,128)(2,1)}, bf16[16,64,128]{2,1,0:T(8,128)(2,1)}) custom-call(bf16[2,4,128,1024]{3,2,1,0:T(8,128)(2,1)} %select_select_fusion.rows, bf16[64,384]{1,0:T(8,128)(2,1)} %copy_bitcast_fusion.2.qkv_s, ...), custom_call_target="tpu_custom_call" | custom-call | tf_op jit(solution)/shard_map/embed_exchange/pallas_call | solution.py:393
  74.8 3.0 %convolution_convert_fusion.4.qkv = bf16[1024,384]{1,0:T(8,128)(2,1)S(1)} fusion(bf16[1024,1024]{1,0:T(8,128)(2,1)} %bitcast.84, bf16[1024,384]{1,0:T(8,128)(2,1)} %bitcast.90), kind=kOutput, calls=%fused_computation.17 | convolution fusion | flops 805699584 | bytes 3670016 | tf_op jit(solution)/shard_map/dot_general | solution.py:712
  79.1 7.9 %attend.1 = (bf16[1024,128]{1,0:T(8,128)(2,1)S(1)}, bf16[128,1024]{1,0:T(8,128)(2,1)S(1)}, bf16[2,1024,1024]{2,1,0:T(8,128)(2,1)S(1)}) custom-call(s32[1]{0:T(128)} %bitcast.2.length, bf16[1024,384]{1,0:T(8,128)(2,1)S(1)} %convolution_convert_fusion.4.qkv), custom_call_target="tpu_custom_call" | custom-call | tf_op jit(solution)/shard_map/attend/pallas_call | solution.py:617
  87.0 1.9 copy-done.1
  89.0 2.1 convolution_convert_fusion.1
  91.0 35.2 %residual_exchange.1 = (bf16[128,1024]{1,0:T(8,128)(2,1)}, bf16[4,2,128,1024]{3,2,1,0:T(8,128)(2,1)}, bf16[16,64,512]{2,1,0:T(8,128)(2,1)}, bf16[16,64,512]{2,1,0:T(8,128)(2,1)}) custom-call(bf16[4,2,128,1024]{3,2,1,0:T(8,128)(2,1)} %bitcast.63, bf16[128,1024]{1,0:T(8,128)(2,1)} %get-tuple-element.33.first, bf16[64,512]{1,0:T(8,128)(2,1)} %up_s.1, ...), custom_call_target="tpu_custom_call" | custom-call | tf_op jit(solution)/shard_map/residual_exchange/pallas_call | solution.py:471
  126.9 5.5 %multiply_reduce_fusion = (f32[512]{0:T(512)}, f32[1024,512]{1,0:T(8,128)}) fusion(f32[1024]{0:T(1024)S(1)} %fusion.7, bf16[1024,1024]{1,0:T(8,128)(2,1)} %bitcast.86, bf16[1024,512]{1,0:T(8,128)(2,1)} %bitcast.88), kind=kOutput, calls=%fused_computation.10 | convolution fusion | flops 1080032768 | bytes 5249024 | tf_op jit(solution)/shard_map/dot_general | solution.py:719
  133.8 11.1 %classify.1 = (f32[1,1024]{1,0:T(1,128)}, f32[1,512]{1,0:T(1,128)}, f32[1,2816]{1,0:T(1,128)}) custom-call(s32[1]{0:T(128)} %bitcast.2.length, s32[1]{0:T(128)} %bitcast.15.label, f32[1,512]{1,0:T(1,128)} %bitcast.83, f32[1,1024]{1,0:T(1,128)} %bitcast.79, bf16[1024,512]{1,0:T(8,128)(2,1)} %bitcast.67, bf16[1024,128]{1,0:T(8,128)(2,1)} %bitcast.73), custom_call_target="tpu_custom_call" | custom-call | tf_op jit(solution)/shard_map/classify/pallas_call | solution.py:565
  145.0 5.6 %convolution_convert_fusion.2 = bf16[1024,512]{1,0:T(8,128)(2,1)} fusion(bf16[1024,1024]{1,0:T(8,128)(2,1)} %bitcast.87, f32[1024,512]{1,0:T(8,128)} %get-tuple-element.67, f32[512]{0:T(512)} %bitcast.91, f32[1024]{0:T(1024)S(1)} %fusion.7), kind=kOutput, calls=%fused_computation.15 | convolution fusion | flops 1084751872 | bytes 5249024 | tf_op jit(solution)/shard_map/pd,pf->df/dot_general | solution.py:727
  150.5 3.6 %convolution_convert_fusion = bf16[1024,1024]{1,0:T(8,128)(2,1)} fusion(bf16[1024,512]{1,0:T(8,128)(2,1)S(1)} %bitcast.89, f32[1024,512]{1,0:T(8,128)S(1)} %copy-done.11, f32[512]{0:T(512)S(1)} %bitcast.92, f32[1024]{0:T(1024)S(1)} %fusion.7), kind=kOutput, calls=%fused_computation.13 | convolution fusion | flops 1085276160 | bytes 5249024 | tf_op jit(solution)/shard_map/pf,df->pd/dot_general | solution.py:728
  155.0 36.5 %backward_exchange.1 = (bf16[4,2,128,1024]{3,2,1,0:T(8,128)(2,1)}, f32[64,512]{1,0:T(8,128)}, f32[16,1,2816]{2,1,0:T(1,128)}) custom-call(bf16[4,2,128,1024]{3,2,1,0:T(8,128)(2,1)} %bitcast.65, bf16[128,1024]{1,0:T(8,128)(2,1)} %get-tuple-element.36.second, f32[128,1024]{1,0:T(8,128)} %broadcast_multiply_fusion.g_third, bf16[16,64,512]{2,1,0:T(8,128)(2,1)} %bitcast.68, ...), custom_call_target="tpu_custom_call" | custom-call | tf_op jit(solution)/shard_map/backward_exchange/pallas_call | solution.py:498
  191.5 2.3 fusion.11.grad
  193.8 8.2 %attend_back.1 = bf16[1024,384]{1,0:T(8,128)(2,1)S(1)} custom-call(bf16[1024,384]{1,0:T(8,128)(2,1)S(1)} %convolution_convert_fusion.4.qkv, bf16[2,1024,1024]{2,1,0:T(8,128)(2,1)} %copy-done.1, bf16[128,1024]{1,0:T(8,128)(2,1)S(1)} %get-tuple-element.45.context_t, f32[1024,128]{1,0:T(8,128)S(1)} %fusion.11.grad), custom_call_target="tpu_custom_call" | custom-call | tf_op jit(solution)/shard_map/attend_back/pallas_call | solution.py:660
  202.1 2.2 convolution_convert_fusion.3
  204.3 1.5 convolution_convert_fusion.5
  206.5 20.9 %collect_gradients.1 = (f32[64,128]{1,0:T(8,128)}, f32[64,384]{1,0:T(8,128)}, f32[512,64]{1,0:T(8,128)}, f32[64,128]{1,0:T(8,128)}, f32[1,128]{1,0:T(1,128)}) custom-call(f32[16,2816]{1,0:T(8,128)} %bitcast.72, bf16[16,64,128]{2,1,0:T(8,128)(2,1)} %bitcast.66, bf16[16,64,384]{2,1,0:T(8,128)(2,1)} %bitcast.71), custom_call_target="tpu_custom_call" | custom-call | tf_op jit(solution)/shard_map/collect_gradients/pallas_call | solution.py:260
  227.3 1.7 copy.20
  229.1 1.5 copy_bitcast_fusion.1
  231.3 1.4 copy.38
  233.3 1.4 copy.40
  (41 shorter events, 8.0 us)
Async XLA Ops:
  0.6 26.2 %copy-start = (bf16[64,3,128]{2,0,1:T(8,128)(2,1)S(1)}, bf16[64,3,128]{2,0,1:T(8,128)(2,1)}, u32[]{:S(2)}) copy-start(bf16[64,3,128]{2,0,1:T(8,128)(2,1)} %param.13) | copy-start | bytes 147460
  74.8 14.2 %copy-start.4 = (bf16[16,64,128]{2,1,0:T(8,128)(2,1)S(1)}, bf16[16,64,128]{2,1,0:T(8,128)(2,1)}, u32[]{:S(2)}) copy-start(bf16[16,64,128]{2,1,0:T(8,128)(2,1)} %get-tuple-element.32) | copy-start | bytes 786436
  87.0 1.9 copy-start.1
  126.9 6.2 %copy-start.3 = (bf16[128,1024]{1,0:T(8,128)(2,1)S(1)}, bf16[128,1024]{1,0:T(8,128)(2,1)}, u32[]{:S(2)}) copy-start(bf16[128,1024]{1,0:T(8,128)(2,1)} %get-tuple-element.36.second) | copy-start | bytes 786436
  144.9 5.6 %copy-start.9 = (bf16[16,64,512]{2,1,0:T(8,128)(2,1)S(1)}, bf16[16,64,512]{2,1,0:T(8,128)(2,1)}, u32[]{:S(2)}) copy-start(bf16[16,64,512]{2,1,0:T(8,128)(2,1)} %get-tuple-element.35) | copy-start | bytes 3145732
  144.9 5.6 %copy-start.10 = (f32[1,512]{1,0:T(1,128)S(1)}, f32[1,512]{1,0:T(1,128)}, u32[]{:S(2)}) copy-start(f32[1,512]{1,0:T(1,128)} %get-tuple-element.39) | copy-start | bytes 6148
  144.9 5.6 %copy-start.11 = (f32[1024,512]{1,0:T(8,128)S(1)}, f32[1024,512]{1,0:T(8,128)}, u32[]{:S(2)}) copy-start(f32[1024,512]{1,0:T(8,128)} %get-tuple-element.67) | copy-start | bytes 6291460
  150.5 3.6 %copy-start.7 = (f32[1,1024]{1,0:T(1,128)S(1)}, f32[1,1024]{1,0:T(1,128)}, u32[]{:S(2)}) copy-start(f32[1,1024]{1,0:T(1,128)} %get-tuple-element.40) | copy-start | bytes 12292
  193.8 8.3 %copy-start.8 = (bf16[4,2,128,1024]{3,2,1,0:T(8,128)(2,1)S(1)}, bf16[4,2,128,1024]{3,2,1,0:T(8,128)(2,1)}, u32[]{:S(2)}) copy-start(bf16[4,2,128,1024]{3,2,1,0:T(8,128)(2,1)} %get-tuple-element.29) | copy-start | bytes 6291460
  202.1 2.2 copy-start.2
  204.3 1.5 copy-start.5
  205.8 26.9 %copy-start.6 = (f32[64,512]{1,0:T(8,128)S(1)}, f32[64,512]{1,0:T(8,128)}, u32[]{:S(2)}) copy-start(f32[64,512]{1,0:T(8,128)} %get-tuple-element.77) | copy-start | bytes 393220

commit v2 on v1

--- a/solution.py
+++ b/solution.py
@@ -253,7 +253,9 @@
     plane.finish(0)
     out_grad[...] = total_of(out_buf)
     plane.finish(1)
-    qkv_grad[...] = total_of(qkv_buf)
+    total = total_of(qkv_buf)
+    for piece in range(3):
+        qkv_grad[:, piece] = total[:, piece * 128 : piece * 128 + 128]
 
 
 def collect(packets, out_term, qkv_term):
@@ -261,7 +263,7 @@
         collect_kernel,
         out_shape=[
             jax.ShapeDtypeStruct((64, 128), F32),
-            jax.ShapeDtypeStruct((64, 384), F32),
+            jax.ShapeDtypeStruct((64, 3, 128), F32),
             jax.ShapeDtypeStruct((512, 64), F32),
             jax.ShapeDtypeStruct((64, 128), F32),
             jax.ShapeDtypeStruct((1, 128), F32),
@@ -483,18 +485,20 @@
     )(terms, first, *shards)
 
 
-def backward_kernel(terms, second, g_third, up_term, packet, g_out, up_grad, packets, up_buf, *scratch):
+def backward_kernel(length, terms, second, per_token, up_term, packet, g_out, up_grad, packets, up_buf, *scratch):
     me, y, c, up, dn, op, oc = ring_places()
     plane = Plane([packet, up_term], [packets, up_buf], *scratch[11:], True)
     grad = pair_sum_to_owner(plane, terms, *scratch[:9])
-    g_out[y, c] = (g_third[...] + normalize_back(second[...].astype(F32), grad)).astype(BF16)
+    live = (y * 2 + c) * 128 + lax.broadcasted_iota(jnp.int32, (128, 1), 0) < length[0]
+    g_third = jnp.where(live, per_token[...], 0.0)
+    g_out[y, c] = (g_third + normalize_back(second[...].astype(F32), grad)).astype(BF16)
     to_all(g_out, *scratch[9:11])
     plane.finish(0)
     plane.finish(1)
     up_grad[...] = total_of(up_buf)
 
 
-def backward(terms, second, g_third, up_term, packet):
+def backward(length, terms, second, per_token, up_term, packet):
     return pl.pallas_call(
         backward_kernel,
         out_shape=[
@@ -502,33 +506,53 @@
             jax.ShapeDtypeStruct((64, 512), F32),
             gathered(packet),
         ],
-        in_specs=[VM] * 5,
+        in_specs=[SM] + [VM] * 5,
         out_specs=[VM] * 3,
         scratch_shapes=[pltpu.VMEM((16, 64, 512), BF16), *PAIR_SCRATCH],
         compiler_params=params(6),
         name="backward_exchange",
-    )(terms, second, g_third, up_term, packet)
+    )(length, terms, second, per_token, up_term, packet)
 
 
 PACKET = 512 + 1024 + 1024 + 128 + 128
-
-
-def head_kernel(
-    length, label, hidden_sum, second_sum, down_t, head, per_token_out, pulled_out, packet_out, parts, send, recv
+ROWS = 256
+LHS_T = (((0,), (0,)), ((), ()))
+RHS_T = (((1,), (1,)), ((), ()))
+
+
+def ffn_kernel(
+    length, label, normed, second, up_w, down_w, head_w, per_token_out, packet_out, terms, up_term,
+    slope, g_pre, parts, send, recv,
 ):
     me, y, c, up, dn, op, oc = ring_places()
     slot = y * 2 + c
-    peers = [(k, e) for k in (0, 1, 3, 2) for e in range(2) if (k, e) != (0, 0)]
+    peers = [(k, e) for k in (2, 1, 3, 0) for e in range(2) if (k, e) != (0, 0)]
 
     def device(k, e):
         return dict(y=add_mod(y, k, 4), c=add_mod(c, e, 2))
 
     for k, e in peers:
         signal(device(4 - k if k else 0, e))
+
+    def live(start, size):
+        return start + lax.broadcasted_iota(jnp.int32, (size, 1), 0) < length[0]
+
+    hidden_sum = jnp.zeros((1, 512), F32)
+    for block in range(1024 // ROWS):
+        rows = pl.ds(block * ROWS, ROWS)
+        hidden = jnp.dot(normed[rows], up_w[...], preferred_element_type=F32)
+        square = hidden * hidden
+        inner = jnp.tanh(0.7978845608028654 * hidden * (1.0 + 0.044715 * square))
+        half = 0.5 * (1.0 + inner)
+        acted = (hidden * half).astype(BF16).astype(F32)
+        slope[rows] = half + 0.5 * hidden * (1.0 - inner * inner) * (
+            0.7978845608028654 + (0.7978845608028654 * 3.0 * 0.044715) * square
+        )
+        hidden_sum += jnp.sum(jnp.where(live(block * ROWS, ROWS), acted, 0.0), axis=0, keepdims=True)
+    own = jnp.where(live(slot * 128, 128), second[...].astype(F32), 0.0)
+    pushed = lax.dot_general(thirds(hidden_sum), down_w[...], RHS_T, preferred_element_type=F32)
+    parts[slot] = jnp.sum(own, axis=0, keepdims=True) + jnp.sum(pushed, axis=0, keepdims=True)
     pl.semaphore_wait(pltpu.get_barrier_semaphore(), 7)
-    contract = (((1,), (1,)), ((), ()))
-    pushed = lax.dot_general(thirds(hidden_sum[...]), down_t[...], contract, preferred_element_type=F32)
-    parts[slot] = second_sum[...] + jnp.sum(pushed, axis=0, keepdims=True)
     steps = [
         remote(parts.at[slot], parts.at[slot], send.at[k, e], recv.at[k, e], device(k, e)) for k, e in peers
     ]
@@ -542,43 +566,56 @@
     count = length[0].astype(F32)
     pooled = pooled / count
     final = normalize(pooled)
-    logits = jnp.sum(jnp.dot(thirds(final), head[...], preferred_element_type=F32), axis=0, keepdims=True)
+    logits = jnp.sum(jnp.dot(thirds(final), head_w[...], preferred_element_type=F32), axis=0, keepdims=True)
     top = jnp.max(logits, axis=-1, keepdims=True)
     total = jnp.log(jnp.sum(jnp.exp(logits - top), axis=-1, keepdims=True)) + top
     labels = (lax.broadcasted_iota(jnp.int32, logits.shape, 1) == label[0]).astype(F32)
     loss = total - jnp.sum(logits * labels, axis=-1, keepdims=True)
     g_logits = (jnp.exp(logits - total) - labels) / 16.0
-    g_final = lax.dot_general(thirds(g_logits), head[...], contract, preferred_element_type=F32)
+    g_final = lax.dot_general(thirds(g_logits), head_w[...], RHS_T, preferred_element_type=F32)
     g_final = jnp.sum(g_final, axis=0, keepdims=True)
     per_token = normalize_back(pooled, g_final) / count
     rounded = per_token.astype(BF16)
+    pulled = jnp.dot(rounded, down_w[...], preferred_element_type=F32)
+    for block in range(1024 // ROWS):
+        rows = pl.ds(block * ROWS, ROWS)
+        grad = jnp.where(live(block * ROWS, ROWS), slope[rows] * pulled, 0.0).astype(BF16)
+        g_pre[rows] = grad
+        terms[rows] = lax.dot_general(grad, up_w[...], RHS_T, preferred_element_type=F32).astype(BF16)
+    for block in range(1024 // ROWS):
+        cols = pl.ds(block * ROWS, ROWS)
+        up_term[cols] = lax.dot_general(
+            normed[:, cols], g_pre[...], LHS_T, preferred_element_type=F32
+        ).astype(BF16)
     per_token_out[...] = per_token
-    pulled_out[...] = jnp.dot(rounded, down_t[...], preferred_element_type=F32)
-    packet_out[:, 0:512] = hidden_sum[...]
+    packet_out[:, 0:512] = hidden_sum
     packet_out[:, 512:1536] = rounded.astype(F32)
     packet_out[:, 1536:2560] = final
     packet_out[:, 2560:2688] = g_logits
     packet_out[:, 2688:2816] = jnp.broadcast_to(loss, (1, 128))
 
 
-def classify(length, label, hidden_sum, second_sum, down_t, head):
+def ffn(length, label, normed, second, up_w, down_w, head_w):
     return pl.pallas_call(
-        head_kernel,
+        ffn_kernel,
         out_shape=[
             jax.ShapeDtypeStruct((1, 1024), F32),
-            jax.ShapeDtypeStruct((1, 512), F32),
             jax.ShapeDtypeStruct((1, PACKET), F32),
-        ],
-        in_specs=[SM, SM, VM, VM, VM, VM],
-        out_specs=[VM, VM, VM],
+            jax.ShapeDtypeStruct((1024, 1024), BF16),
+            jax.ShapeDtypeStruct((1024, 512), BF16),
+        ],
+        in_specs=[SM, SM, VM, VM, VM, VM, VM],
+        out_specs=[VM, VM, VM, VM],
         scratch_shapes=[
+            pltpu.VMEM((1024, 512), F32),
+            pltpu.VMEM((1024, 512), BF16),
             pltpu.VMEM((8, 1, 1024), F32),
             pltpu.SemaphoreType.DMA((4, 2)),
             pltpu.SemaphoreType.DMA((4, 2)),
         ],
         compiler_params=params(7),
-        name="classify",
-    )(length, label, hidden_sum, second_sum, down_t, head)
+        name="ffn",
+    )(length, label, normed, second, up_w, down_w, head_w)
 
 
 SCALE = 0.125
@@ -595,45 +632,57 @@
     return jnp.where((cols >= 64) == (head == 1), value, jnp.zeros_like(value))
 
 
-def attend_kernel(length, qkv, context, context_t, probs_t):
+def attend_kernel(length, normed, qkv_w, out_w, qkv, context_t, probs_t, terms):
+    for block in range(4):
+        rows = pl.ds(block * 256, 256)
+        qkv[rows] = jnp.dot(normed[rows], qkv_w[...], preferred_element_type=F32).astype(BF16)
     keys = qkv[:, 128:256]
-    query_t = qkv[:, 0:128].T
+    query_t = (qkv[:, 0:128] * SCALE).T
     values_t = qkv[:, 256:384].T
+    out_t = out_w[...].T
     seen = lax.broadcasted_iota(jnp.int32, (1024, WIDE), 0) < length[0]
     for block in range(1024 // WIDE):
         cols = slice(block * WIDE, (block + 1) * WIDE)
         for head in range(2):
-            scores = jnp.dot(keys, head_rows(query_t[:, cols], head), preferred_element_type=F32) * SCALE
+            scores = jnp.dot(keys, head_rows(query_t[:, cols], head), preferred_element_type=F32)
             scores = jnp.where(seen, scores, -1e30)
             expo = jnp.exp(scores - jnp.max(scores, axis=0, keepdims=True))
             probs = (expo * (1.0 / jnp.sum(expo, axis=0, keepdims=True))).astype(BF16)
             probs_t[head, :, cols] = probs
             rows = slice(head * 64, head * 64 + 64)
             context_t[rows, cols] = jnp.dot(values_t[rows], probs, preferred_element_type=F32).astype(BF16)
-    context[...] = context_t[...].T
-
-
-def attend(length, qkv):
+        terms[cols] = jnp.dot(context_t[:, cols].T, out_t, preferred_element_type=F32).astype(BF16)
+
+
+def attend(length, normed, qkv_w, out_w):
     return pl.pallas_call(
         attend_kernel,
         out_shape=[
-            jax.ShapeDtypeStruct((1024, 128), BF16),
+            jax.ShapeDtypeStruct((1024, 384), BF16),
             jax.ShapeDtypeStruct((128, 1024), BF16),
             jax.ShapeDtypeStruct((2, 1024, 1024), BF16),
-        ],
-        in_specs=[SM, VM],
-        out_specs=[VM, VM, VM],
+            jax.ShapeDtypeStruct((1024, 1024), BF16),
+        ],
+        in_specs=[SM, VM, VM, VM],
+        out_specs=[VM] * 4,
         compiler_params=pltpu.CompilerParams(vmem_limit_bytes=48 * 2**20),
         name="attend",
-    )(length, qkv)
-
-
-def attend_back_kernel(qkv, probs_t, context_t, grad, out, grad_q, grad_k, grad_v):
-    query = qkv[:, 0:128]
-    keys_t = qkv[:, 128:256].T
+    )(length, normed, qkv_w, out_w)
+
+
+def attend_back_kernel(
+    g_second, normed, out_w, qkv, probs_t, context_t, out_term, qkv_term, grad, grad_t, grad_q, grad_k, grad_v
+):
+    out_term[...] = jnp.dot(context_t[...], g_second[...], preferred_element_type=F32).T.astype(BF16)
+    for block in range(4):
+        rows = pl.ds(block * 256, 256)
+        part = jnp.dot(g_second[rows], out_w[...], preferred_element_type=F32)
+        grad[rows] = part.astype(BF16)
+        grad_t[:, block * 256 : block * 256 + 256] = part.T
+    query = qkv[:, 0:128] * SCALE
+    keys_t = (qkv[:, 128:256] * SCALE).T
     values = qkv[:, 256:384]
-    grad_t = grad[...].T
-    product = grad_t * context_t[...].astype(F32)
+    product = grad_t[...] * context_t[...].astype(F32)
     for block in range(1024 // WIDE):
         cols = slice(block * WIDE, (block + 1) * WIDE)
         for head in range(2):
@@ -641,47 +690,41 @@
             probs = probs_t[head, :, cols]
             delta = jnp.sum(product[rows, cols], axis=0, keepdims=True)
             pulled = jnp.dot(values, head_rows(grad_t[:, cols], head).astype(BF16), preferred_element_type=F32)
-            g_scores = (probs.astype(F32) * (pulled - delta) * SCALE).astype(BF16)
-            grad_q[rows, cols] = jnp.dot(keys_t[rows], g_scores, preferred_element_type=F32)
+            g_scores = (probs.astype(F32) * (pulled - delta)).astype(BF16)
+            grad_q[rows, cols] = jnp.dot(keys_t[rows], g_scores, preferred_element_type=F32).astype(BF16)
             g_keys = jnp.dot(g_scores, head_cols(query[cols], head), preferred_element_type=F32)
-            g_vals = jnp.dot(probs, head_cols(grad[cols], head).astype(BF16), preferred_element_type=F32)
+            g_vals = jnp.dot(probs, head_cols(grad[cols], head), preferred_element_type=F32)
             if block == 0 and head == 0:
                 grad_k[...] = g_keys
                 grad_v[...] = g_vals
             else:
                 grad_k[...] += g_keys
                 grad_v[...] += g_vals
-    out[:, 0:128] = grad_q[...].T.astype(BF16)
-    out[:, 128:256] = grad_k[...].astype(BF16)
-    out[:, 256:384] = grad_v[...].astype(BF16)
-
-
-def attend_back(qkv, probs_t, context_t, grad):
+    for piece, value in enumerate((None, grad_k, grad_v)):
+        left = grad_q[...] if value is None else value[...].T.astype(BF16)
+        part = jnp.dot(left, normed[...], preferred_element_type=F32)
+        qkv_term[:, piece * 128 : piece * 128 + 128] = part.T.astype(BF16)
+
+
+def attend_back(g_second, normed, out_w, qkv, probs_t, context_t):
     return pl.pallas_call(
         attend_back_kernel,
-        out_shape=jax.ShapeDtypeStruct((1024, 384), BF16),
-        in_specs=[VM, VM, VM, VM],
-        out_specs=VM,
+        out_shape=[
+            jax.ShapeDtypeStruct((1024, 128), BF16),
+            jax.ShapeDtypeStruct((1024, 384), BF16),
+        ],
+        in_specs=[VM] * 6,
+        out_specs=[VM] * 2,
         scratch_shapes=[
+            pltpu.VMEM((1024, 128), BF16),
             pltpu.VMEM((128, 1024), F32),
+            pltpu.VMEM((128, 1024), BF16),
             pltpu.VMEM((1024, 128), F32),
             pltpu.VMEM((1024, 128), F32),
         ],
         compiler_params=pltpu.CompilerParams(vmem_limit_bytes=48 * 2**20),
         name="attend_back",
-    )(qkv, probs_t, context_t, grad)
-
-
-def gelu(values):
-    inner = jnp.tanh(0.7978845608028654 * (values + 0.044715 * values * values * values))
-    return 0.5 * values * (1.0 + inner)
-
-
-def gelu_slope(values):
-    inner = jnp.tanh(0.7978845608028654 * (values + 0.044715 * values * values * values))
-    return 0.5 * (1.0 + inner) + 0.5 * values * (1.0 - inner * inner) * 0.7978845608028654 * (
-        1.0 + 3.0 * 0.044715 * values * values
-    )
+    )(g_second, normed, out_w, qkv, probs_t, context_t)
 
 
 def per_device(token_ids, lengths, teacher_bins, table, qkv_shard, out_shard, up_shard, down_shard, head_shard):
@@ -709,35 +752,21 @@
     out_w = out_w.reshape(1024, 128)
     head_w = head_w.reshape(1024, 128)
     normed = normed.reshape(1024, 1024)
-    qkv = jnp.dot(normed, qkv_w, preferred_element_type=F32).astype(BF16)
-    context, context_t, probs_t = attend(length, qkv)
-    terms = jnp.einsum("ph,dh->pd", context, out_w, preferred_element_type=F32).astype(BF16)
+    qkv, context_t, probs_t, terms = attend(length, normed, qkv_w, out_w)
     second, normed_two, up_w, down_w = residual(terms.reshape(4, 2, 128, 1024), first, [up_shard, down_shard.T])
     up_w = up_w.reshape(1024, 512)
     down_w = down_w.reshape(1024, 512)
-    normed_two = normed_two.reshape(1024, 1024)
-    hidden = jnp.dot(normed_two, up_w, preferred_element_type=F32)
-    live = (jnp.arange(1024, dtype=jnp.int32)[:, None] < length[0]).astype(F32)
-    own = (me["y"] * 2 + me["c"]) * 128 + jnp.arange(128, dtype=jnp.int32)[:, None]
-    live_own = (own < length[0]).astype(F32)
-    hidden_sum = jnp.sum(gelu(hidden).astype(BF16).astype(F32) * live, axis=0, keepdims=True)
-    second_sum = jnp.sum(second.astype(F32) * live_own, axis=0, keepdims=True)
-    per_token, pulled, packet = classify(length, label, hidden_sum, second_sum, down_w, head_w)
-    g_pre = (gelu_slope(hidden) * (pulled * live)).astype(BF16)
-    up_term = jnp.einsum("pd,pf->df", normed_two, g_pre, preferred_element_type=F32).astype(BF16)
-    terms = jnp.einsum("pf,df->pd", g_pre, up_w, preferred_element_type=F32).astype(BF16)
+    per_token, packet, terms, up_term = ffn(
+        length, label, normed_two.reshape(1024, 1024), second, up_w, down_w, head_w
+    )
     g_second, up_grad, packets = backward(
-        terms.reshape(4, 2, 128, 1024), second, per_token * live_own, up_term.reshape(16, 64, 512), packet
-    )
-    g_second = g_second.reshape(1024, 1024)
-    out_term = jnp.einsum("pd,ph->dh", g_second, context, preferred_element_type=F32).astype(BF16)
-    g_context = jnp.einsum("pd,dh->ph", g_second, out_w, preferred_element_type=F32)
-    g_qkv = attend_back(qkv, probs_t, context_t, g_context)
-    qkv_term = jnp.einsum("pd,pr->dr", normed, g_qkv, preferred_element_type=F32).astype(BF16)
+        length, terms.reshape(4, 2, 128, 1024), second, per_token, up_term.reshape(16, 64, 512), packet
+    )
+    out_term, qkv_term = attend_back(g_second.reshape(1024, 1024), normed, out_w, qkv, probs_t, context_t)
     out_grad, qkv_grad, down_grad, head_grad, loss = collect(
         packets.reshape(16, PACKET), out_term.reshape(16, 64, 128), qkv_term.reshape(16, 64, 384)
     )
-    return loss[0, 0], qkv_grad.reshape(64, 3, 128), out_grad.T, up_grad, down_grad, head_grad
+    return loss[0, 0], qkv_grad, out_grad.T, up_grad, down_grad, head_grad
 
 
 def solution(mesh):

time: 237 us -> 227 us (0.958)
  matrix products: 25.8 us -> 0 us
  Pallas kernels: 178 us -> 191 us
  local copies, waits for them, and re-layouts: 20.7 us -> 26.2 us
  other arithmetic: 7.38 us -> 4.43 us
    dot_general x8 -> x0, matrix products: 25.8 us -> none  [the longest x1 5.56 us: per_device(): jnp.einsum('pd,pf->df', normed_two, g_pre, preferred_element_type=F32)]
    pallas_call x3, Pallas kernels: 27.2 us -> 39.8 us  [the longest x1 16.2 us: ffn(): pl.pallas_call(ffn_kernel, out_shape=[jax.ShapeDtypeStruct((1, 1024), F32...]
    unnamed x31 -> x25, local copies, waits for them, and re-layouts: 9.34 us -> 14.9 us
where the time goes in v2:
time: 227 us; the launch traced here: 226 us
  Pallas kernels  191 us (84%)
  local copies, waits for them, and re-layouts  26.2 us (12%)
  other arithmetic  4.43 us (2%)
  between operations  3.83 us (2%)
    pallas_call x1, Pallas kernels, embed(): pl.pallas_call(embed_kernel, out_shape=[jax.ShapeDtypeStruct((128, 1024),...  47.3 us
    pallas_call x1, Pallas kernels, backward(): pl.pallas_call(backward_kernel, out_shape=[jax.ShapeDtypeStruct((4, 2, 12...  37.2 us
    pallas_call x1, Pallas kernels, residual(): pl.pallas_call(residual_kernel, out_shape=[jax.ShapeDtypeStruct((128, 102...  35.3 us
    pallas_call x1, Pallas kernels, collect(): pl.pallas_call(collect_kernel, out_shape=[jax.ShapeDtypeStruct((64, 128),...  20.7 us
    pallas_call x1, Pallas kernels, ffn(): pl.pallas_call(ffn_kernel, out_shape=[jax.ShapeDtypeStruct((1, 1024), F32...  16.2 us
    unnamed x25, local copies, waits for them, and re-layouts  14.9 us
    pallas_call x1, Pallas kernels, attend(): pl.pallas_call(attend_kernel, out_shape=[jax.ShapeDtypeStruct((1024, 384)...  13.1 us
    pallas_call x1, Pallas kernels, spread_ids(): pl.pallas_call(spread_ids_kernel, out_shape=jax.ShapeDtypeStruct((2, 4, 8...  10.9 us

profile of v2, /device:TPU:1, one launch (start us, length us, event | category | flops | bytes accessed | tf_op | source)
XLA Modules:
  0.0 225.7 jit_solution(7025606275006325087)
XLA Ops:
  2.2 1.3 add_add_fusion.src
  3.5 10.9 %spread_ids.1 = s32[2,4,8,128]{3,2,1,0:T(8,128)} custom-call(s32[8,128]{1,0:T(8,128)} %add_add_fusion.src), custom_call_target="tpu_custom_call" | custom-call | tf_op jit(solution)/shard_map/spread_ids/pallas_call | solution.py:114
  14.4 1.3 fusion
  15.7 0.8 broadcast_clamp_fusion.1
  16.5 0.8 compare_and_fusion
  18.0 9.2 %gather_fusion = bf16[1024,1024]{1,0:T(8,128)(2,1)S(1)} fusion(bf16[3816,1024]{1,0:T(8,128)(2,1)} %param.12, s32[1024]{0:T(1024)S(1)} %broadcast_clamp_fusion), kind=kCustom, calls=%fused_computation | custom fusion | bytes 4198400 | tf_op jit(solution)/shard_map/jit(_take)/gather | solution.py:748
  27.2 1.6 select_select_fusion.rows
  28.7 47.3 %embed_exchange.1 = (bf16[128,1024]{1,0:T(8,128)(2,1)}, bf16[4,2,128,1024]{3,2,1,0:T(8,128)(2,1)}, bf16[16,64,384]{2,1,0:T(8,128)(2,1)}, bf16[16,64,128]{2,1,0:T(8,128)(2,1)}, bf16[16,64,128]{2,1,0:T(8,128)(2,1)}) custom-call(bf16[2,4,128,1024]{3,2,1,0:T(8,128)(2,1)} %select_select_fusion.rows, bf16[64,384]{1,0:T(8,128)(2,1)} %copy_bitcast_fusion.1.qkv_s, ...), custom_call_target="tpu_custom_call" | custom-call | tf_op jit(solution)/shard_map/embed_exchange/pallas_call | solution.py:395
  76.1 0.9 copy-done.3
  77.0 1.1 copy-done.6
  78.1 13.1 %attend.1 = (bf16[1024,384]{1,0:T(8,128)(2,1)S(1)}, bf16[128,1024]{1,0:T(8,128)(2,1)S(1)}, bf16[2,1024,1024]{2,1,0:T(8,128)(2,1)}, bf16[1024,1024]{1,0:T(8,128)(2,1)S(1)}) custom-call(s32[1]{0:T(128)} %bitcast.2.length, bf16[1024,1024]{1,0:T(8,128)(2,1)} %bitcast.44, bf16[1024,384]{1,0:T(8,128)(2,1)S(1)} %bitcast.42, bf16[1024,128]{1,0:T(8,128)(2,1)S(1)} %bitcast.39), custom_call_target="tpu_custom_call" | custom-call | tf_op jit(solution)/shard_map/attend/pallas_call | solution.py:658
  91.2 1.4 copy-done.2
  92.6 35.3 %residual_exchange.1 = (bf16[128,1024]{1,0:T(8,128)(2,1)}, bf16[4,2,128,1024]{3,2,1,0:T(8,128)(2,1)}, bf16[16,64,512]{2,1,0:T(8,128)(2,1)}, bf16[16,64,512]{2,1,0:T(8,128)(2,1)}) custom-call(bf16[4,2,128,1024]{3,2,1,0:T(8,128)(2,1)} %bitcast.38, bf16[128,1024]{1,0:T(8,128)(2,1)} %get-tuple-element.37.first, bf16[64,512]{1,0:T(8,128)(2,1)} %up_s.1, ...), custom_call_target="tpu_custom_call" | custom-call | tf_op jit(solution)/shard_map/residual_exchange/pallas_call | solution.py:473
  127.9 16.2 %ffn.1 = (f32[1,1024]{1,0:T(1,128)}, f32[1,2816]{1,0:T(1,128)}, bf16[1024,1024]{1,0:T(8,128)(2,1)}, bf16[1024,512]{1,0:T(8,128)(2,1)}) custom-call(s32[1]{0:T(128)} %bitcast.2.length, s32[1]{0:T(128)} %bitcast.3.label, bf16[1024,1024]{1,0:T(8,128)(2,1)} %bitcast.47, bf16[128,1024]{1,0:T(8,128)(2,1)} %get-tuple-element.39.second, bf16[1024,512]{1,0:T(8,128)(2,1)} %bitcast.50, ...), custom_call_target="tpu_custom_call" | custom-call | tf_op jit(solution)/shard_map/ffn/pallas_call | solution.py:599
  144.1 37.2 %backward_exchange.1 = (bf16[4,2,128,1024]{3,2,1,0:T(8,128)(2,1)}, f32[64,512]{1,0:T(8,128)}, f32[16,1,2816]{2,1,0:T(1,128)}) custom-call(s32[1]{0:T(128)} %bitcast.2.length, bf16[4,2,128,1024]{3,2,1,0:T(8,128)(2,1)} %bitcast.48, bf16[128,1024]{1,0:T(8,128)(2,1)} %get-tuple-element.39.second, f32[1,1024]{1,0:T(1,128)} %get-tuple-element.44.per_token, ...), custom_call_target="tpu_custom_call" | custom-call | tf_op jit(solution)/shard_map/backward_exchange/pallas_call | solution.py:502
  181.3 1.6 copy.27
  182.9 1.6 copy-done.1
  184.5 10.5 %attend_back.1 = (bf16[1024,128]{1,0:T(8,128)(2,1)S(1)}, bf16[1024,384]{1,0:T(8,128)(2,1)S(1)}) custom-call(bf16[1024,1024]{1,0:T(8,128)(2,1)S(1)} %bitcast.37, bf16[1024,1024]{1,0:T(8,128)(2,1)} %bitcast.45, bf16[1024,128]{1,0:T(8,128)(2,1)S(1)} %bitcast.40, bf16[1024,384]{1,0:T(8,128)(2,1)S(1)} %get-tuple-element.49.qkv, ...), custom_call_target="tpu_custom_call" | custom-call | tf_op jit(solution)/shard_map/attend_back/pallas_call | solution.py:710
  195.0 0.9 copy-done.5
  196.6 20.7 %collect_gradients.1 = (f32[64,128]{1,0:T(8,128)}, f32[64,3,128]{2,1,0:T(4,128)}, f32[512,64]{1,0:T(8,128)}, f32[64,128]{1,0:T(8,128)}, f32[1,128]{1,0:T(1,128)}) custom-call(f32[16,2816]{1,0:T(8,128)} %bitcast.52, bf16[16,64,128]{2,1,0:T(8,128)(2,1)} %bitcast.43, bf16[16,64,384]{2,1,0:T(8,128)(2,1)} %bitcast.41), custom_call_target="tpu_custom_call" | custom-call | tf_op jit(solution)/shard_map/collect_gradients/pallas_call | solution.py:262
  217.3 1.6 copy.19
  218.9 1.7 copy.20
  221.2 1.4 copy.36
  223.2 1.4 copy.38
  (23 shorter events, 2.3 us)
Async XLA Ops:
  0.6 16.7 %copy-start = (bf16[64,3,128]{2,0,1:T(8,128)(2,1)S(1)}, bf16[64,3,128]{2,0,1:T(8,128)(2,1)}, u32[]{:S(2)}) copy-start(bf16[64,3,128]{2,0,1:T(8,128)(2,1)} %param.13) | copy-start | bytes 147460
  76.1 1.0 copy-start.3
  77.0 1.1 copy-start.6
  91.2 1.4 copy-start.2
  144.1 38.9 %copy-start.4 = (bf16[16,64,128]{2,1,0:T(8,128)(2,1)S(1)}, bf16[16,64,128]{2,1,0:T(8,128)(2,1)}, u32[]{:S(2)}) copy-start(bf16[16,64,128]{2,1,0:T(8,128)(2,1)} %get-tuple-element.35) | copy-start | bytes 786436
  182.9 1.6 copy-start.1
  184.5 38.1 %copy-start.8 = (f32[64,512]{1,0:T(8,128)S(1)}, f32[64,512]{1,0:T(8,128)}, u32[]{:S(2)}) copy-start(f32[64,512]{1,0:T(8,128)} %get-tuple-element.83) | copy-start | bytes 393220
  195.0 0.9 copy-start.5
  195.9 0.7 copy-start.7

commit v3 on v2

--- a/solution.py
+++ b/solution.py
@@ -25,8 +25,10 @@
     return lax.rem(value + step, size)
 
 
-def params(number):
-    return pltpu.CompilerParams(collective_id=number, has_side_effects=True)
+def params(number, mebibytes):
+    return pltpu.CompilerParams(
+        collective_id=number, has_side_effects=True, vmem_limit_bytes=mebibytes * 2**20
+    )
 
 
 def remote(src, dst, send, recv, device):
@@ -57,69 +59,81 @@
     )
 
 
-def spread_ids_kernel(src, out, send, recv):
-    me = where_am_i()
-    xl, z, c, y, xh = (me[n] for n in ("xl", "z", "c", "y", "xh"))
-    here = xh == c
-
-    for role in range(2):
+class Ids:
+    def __init__(self, src, out, send, recv):
+        self.src, self.out, self.send, self.recv = src, out, send, recv
+        self.me = where_am_i()
+        self.here = self.me["xh"] == self.me["c"]
+
+    def greet(self):
+        me = self.me
+        for role in range(2):
+            for k in range(4):
+                source = dict(
+                    xl=add_mod(me["xl"], role, 2),
+                    c=add_mod(me["xh"], role, 2),
+                    xh=me["c"],
+                    y=add_mod(me["y"], 4 - k, 4),
+                    z=me["z"],
+                )
+                if role == 0 and k == 0:
+
+                    @pl.when(jnp.logical_not(self.here))
+                    def _(source=source):
+                        signal(source)
+                else:
+                    signal(source)
+        return jnp.where(self.here, 7, 8)
+
+    def copy(self, role, k):
+        me = self.me
+        return remote(
+            self.src,
+            self.out.at[role, me["y"]],
+            self.send.at[role, k],
+            self.recv.at[role, k],
+            dict(
+                xl=add_mod(me["xl"], role, 2),
+                c=me["xh"],
+                xh=add_mod(me["c"], role, 2),
+                y=add_mod(me["y"], k, 4),
+                z=me["z"],
+            ),
+        )
+
+    def local(self):
+        return pltpu.make_async_copy(self.src, self.out.at[0, self.me["y"]], self.recv.at[0, 0])
+
+    def start(self):
+        for role in (1, 0):
+            for k in (2, 1, 3, 0):
+                if role == 0 and k == 0:
+
+                    @pl.when(jnp.logical_not(self.here))
+                    def _():
+                        self.copy(0, 0).start()
+
+                    @pl.when(self.here)
+                    def _():
+                        self.local().start()
+                else:
+                    self.copy(role, k).start()
+
+    def arrive(self, role):
         for k in range(4):
-            source = dict(
-                xl=add_mod(xl, role, 2), c=add_mod(xh, role, 2), xh=c, y=add_mod(y, 4 - k, 4), z=z
-            )
-            if role == 0 and k == 0:
-
-                @pl.when(jnp.logical_not(here))
-                def _(source=source):
-                    signal(source)
-            else:
-                signal(source)
-    pl.semaphore_wait(pltpu.get_barrier_semaphore(), jnp.where(here, 7, 8))
-
-    def copy(role, k):
-        return remote(
-            src,
-            out.at[role, y],
-            send.at[role, k],
-            recv.at[role, k],
-            dict(xl=add_mod(xl, role, 2), c=xh, xh=add_mod(c, role, 2), y=add_mod(y, k, 4), z=z),
-        )
-
-    for role in range(2):
-        for k in range(4):
-            if role == 0 and k == 0:
-
-                @pl.when(jnp.logical_not(here))
-                def _():
-                    copy(0, 0).start()
-
-                @pl.when(here)
-                def _():
-                    pltpu.make_async_copy(src, out.at[0, y], recv.at[0, 0]).start()
-            else:
-                copy(role, k).start()
-    for role in range(2):
-        for k in range(4):
-            if role == 0 and k == 0:
-
-                @pl.when(jnp.logical_not(here))
-                def _():
-                    copy(0, 0).wait_send()
-            else:
-                copy(role, k).wait_send()
-            pltpu.make_async_copy(src, out.at[role, add_mod(y, 4 - k, 4)], recv.at[role, k]).wait()
-
-
-def spread_ids(packet):
-    return pl.pallas_call(
-        spread_ids_kernel,
-        out_shape=jax.ShapeDtypeStruct((2, 4, 8, 128), jnp.int32),
-        in_specs=[VM],
-        out_specs=VM,
-        scratch_shapes=[pltpu.SemaphoreType.DMA((2, 4)), pltpu.SemaphoreType.DMA((2, 4))],
-        compiler_params=params(1),
-        name="spread_ids",
-    )(packet)
+            place = add_mod(self.me["y"], 4 - k, 4)
+            pltpu.make_async_copy(self.src, self.out.at[role, place], self.recv.at[role, k]).wait()
+
+    def sent(self):
+        for role in range(2):
+            for k in range(4):
+                if role == 0 and k == 0:
+
+                    @pl.when(jnp.logical_not(self.here))
+                    def _():
+                        self.copy(0, 0).wait_send()
+                else:
+                    self.copy(role, k).wait_send()
 
 
 class Plane:
@@ -271,7 +285,7 @@
         in_specs=[VM] * 3,
         out_specs=[VM] * 5,
         scratch_shapes=[pltpu.VMEM((16, 64, 128), BF16), pltpu.VMEM((16, 64, 384), BF16), *plane_sems(2)],
-        compiler_params=params(3),
+        compiler_params=params(3, 16),
         name="collect_gradients",
     )(packets, out_term, qkv_term)
 
@@ -285,30 +299,31 @@
 HALVES = (pl.ds(0, 64), pl.ds(64, 64))
 
 
-def to_owner(blocks, stage, far, near, send, recv, meanwhile=None):
+def to_owner(blocks, stage, far, near, send, recv):
     me, y, c, up, dn, op, oc = ring_places()
     first = [
         remote(blocks(op).at[HALVES[0]], far.at[0], send.at[0], recv.at[0], dict(y=up)),
         remote(blocks(op).at[HALVES[1]], far.at[1], send.at[1], recv.at[1], dict(y=dn)),
     ]
-    for step in first:
-        step.start()
-    if meanwhile is not None:
-        meanwhile()
 
     def second(side):
         return remote(
             stage.at[side], near.at[side], send.at[2 + side], recv.at[2 + side], dict(y=(up, dn)[side])
         )
 
-    stage[0, 64:128] = blocks(up)[64:128]
-    stage[1, 0:64] = blocks(dn)[0:64]
-    first[0].wait_recv()
-    stage[0, 0:64] = (blocks(up)[0:64].astype(F32) + far[0].astype(F32)).astype(BF16)
-    second(0).start()
-    first[1].wait_recv()
-    stage[1, 64:128] = (blocks(dn)[64:128].astype(F32) + far[1].astype(F32)).astype(BF16)
-    second(1).start()
+    def begin():
+        for step in first:
+            step.start()
+
+    def relay():
+        stage[0, 64:128] = blocks(up)[64:128]
+        stage[1, 0:64] = blocks(dn)[0:64]
+        first[0].wait_recv()
+        stage[0, 0:64] = (blocks(up)[0:64].astype(F32) + far[0].astype(F32)).astype(BF16)
+        second(0).start()
+        first[1].wait_recv()
+        stage[1, 64:128] = (blocks(dn)[64:128].astype(F32) + far[1].astype(F32)).astype(BF16)
+        second(1).start()
 
     def finish():
         for step in first:
@@ -317,7 +332,7 @@
         second(1).wait()
         return blocks(y)[...].astype(F32) + near[0].astype(F32) + near[1].astype(F32)
 
-    return finish
+    return begin, relay, finish
 
 
 def to_all(out, send, recv):
@@ -357,16 +372,49 @@
 
 
 def embed_kernel(
-    rows, qkv_s, out_s, head_s, first_out, normed_out, qkv_w, out_w, head_w,
-    stage, far, near, other, total, rsend, rrecv, asend, arecv, psend, precv,
+    count, label, ids, table, qkv_s, out_s, head_s, info, first_out, normed_out, qkv_w, out_w, head_w,
+    packet, got, shard, chosen, rows, stage, far, near, other, total,
+    load, isend, irecv, rsend, rrecv, asend, arecv, psend, precv,
 ):
     me, y, c, up, dn, op, oc = ring_places()
+    vocab = table.shape[0]
+    padded = shard.shape[0]
+    fetch = pltpu.make_async_copy(table, shard.at[pl.ds(0, vocab)], load)
+    fetch.start()
+    tokens = Ids(packet, got, isend, irecv)
     plane = Plane([qkv_s, out_s, head_s], [qkv_w, out_w, head_w], psend, precv, False)
     partner = dict(xl=1 - me["xl"], xh=1 - me["xh"])
     for device in (dict(y=up), dict(y=dn), dict(c=oc), partner):
         signal(device)
-    pl.semaphore_wait(pltpu.get_barrier_semaphore(), plane.greet() + 4)
-    done = [
+    greeted = tokens.greet() + plane.greet() + 4
+    line = lax.broadcasted_iota(jnp.int32, (8, 128), 0)
+    packet[...] = jnp.where(line == 0, ids[...], jnp.where(line == 1, count[0], label[0]))
+    if padded > vocab:
+        shard[vocab:padded] = jnp.zeros((padded - vocab, shard.shape[1]), BF16)
+    pl.semaphore_wait(pltpu.get_barrier_semaphore(), greeted)
+    tokens.start()
+    for i in range(3):
+        plane.start(i)
+    base = (y * 2 + me["xh"]) * vocab
+    lanes = lax.broadcasted_iota(jnp.int32, (128, 128), 1)
+
+    def look_up(role):
+        tokens.arrive(role)
+        for b in range(4):
+            wanted = jnp.broadcast_to(got[role, b, 0:1, :], (128, 128)).T - base
+            for tile in range(padded // 128):
+                chosen[b * 128 : b * 128 + 128, tile * 128 : tile * 128 + 128] = jnp.where(
+                    wanted == lanes + tile * 128, 1.0, 0.0
+                ).astype(BF16)
+        if role == 1:
+            fetch.wait()
+        for part in range(4):
+            cols = slice(part * 256, part * 256 + 256)
+            found = jnp.dot(chosen[...], shard[:, cols], preferred_element_type=F32).astype(BF16)
+            for b in range(4):
+                rows[role, b, :, cols] = found[b * 128 : b * 128 + 128]
+
+    owner = [
         to_owner(
             lambda b, role=role: rows.at[role, b],
             stage.at[role],
@@ -374,14 +422,20 @@
             near.at[role],
             rsend.at[role],
             rrecv.at[role],
-            (lambda: [plane.start(i) for i in range(3)]) if role == 1 else None,
         )
-        for role in (1, 0)
+        for role in range(2)
     ]
-    total[...] = done[0]().astype(BF16)
+    look_up(1)
+    owner[1][0]()
+    look_up(0)
+    owner[0][0]()
+    info[...] = got[0, 0]
+    owner[1][1]()
+    owner[0][1]()
+    total[...] = owner[1][2]().astype(BF16)
     cross = remote(total, other, rsend.at[2, 0], rrecv.at[2, 0], partner)
     cross.start()
-    mine = done[1]()
+    mine = owner[0][2]()
     cross.wait()
     first = mine + other[...].astype(F32)
     first_out[...] = first.astype(BF16)
@@ -389,33 +443,44 @@
     to_all(normed_out, asend, arecv)
     for i in range(3):
         plane.finish(i)
-
-
-def embed(rows, shards):
+    tokens.sent()
+
+
+def embed(count, label, ids, table, shards):
+    padded = -(-table.shape[0] // 256) * 256
     return pl.pallas_call(
         embed_kernel,
         out_shape=[
+            jax.ShapeDtypeStruct((8, 128), jnp.int32),
             jax.ShapeDtypeStruct((128, 1024), BF16),
             jax.ShapeDtypeStruct((4, 2, 128, 1024), BF16),
             *map(gathered, shards),
         ],
-        in_specs=[VM] * 4,
-        out_specs=[VM] * 5,
+        in_specs=[SM, SM, VM, pl.BlockSpec(memory_space=pl.ANY), VM, VM, VM],
+        out_specs=[VM] * 6,
         scratch_shapes=[
+            pltpu.VMEM((8, 128), jnp.int32),
+            pltpu.VMEM((2, 4, 8, 128), jnp.int32),
+            pltpu.VMEM((padded, 1024), BF16),
+            pltpu.VMEM((512, padded), BF16),
+            pltpu.VMEM((2, 4, 128, 1024), BF16),
             pltpu.VMEM((2, 2, 128, 1024), BF16),
             pltpu.VMEM((2, 2, 64, 1024), BF16),
             pltpu.VMEM((2, 2, 128, 1024), BF16),
             pltpu.VMEM((128, 1024), BF16),
             pltpu.VMEM((128, 1024), BF16),
+            pltpu.SemaphoreType.DMA,
+            pltpu.SemaphoreType.DMA((2, 4)),
+            pltpu.SemaphoreType.DMA((2, 4)),
             pltpu.SemaphoreType.DMA((3, 4)),
             pltpu.SemaphoreType.DMA((3, 4)),
             pltpu.SemaphoreType.DMA((9,)),
             pltpu.SemaphoreType.DMA((9,)),
             *plane_sems(3),
         ],
-        compiler_params=params(4),
+        compiler_params=params(4, 40),
         name="embed_exchange",
-    )(rows, *shards)
+    )(count, label, ids, table, *shards)
 
 
 def pair_sum_to_owner(plane, terms, pair, summed, stage, far, near, psend, precv, rsend, rrecv):
@@ -432,10 +497,14 @@
         step.start()
     for i in range(len(plane.srcs)):
         plane.start(i)
+    begin, relay, finish = to_owner(lambda b: summed.at[b], stage, far, near, rsend, rrecv)
     for i, b in enumerate(order):
         steps[i].wait_recv()
         summed[b] = (terms[b, c].astype(F32) + pair[b].astype(F32)).astype(BF16)
-    total = to_owner(lambda b: summed.at[b], stage, far, near, rsend, rrecv)()
+        if i == 0:
+            begin()
+    relay()
+    total = finish()
     for step in steps:
         step.wait_send()
     return total
@@ -480,16 +549,16 @@
         in_specs=[VM] * 4,
         out_specs=[VM] * 4,
         scratch_shapes=PAIR_SCRATCH,
-        compiler_params=params(5),
+        compiler_params=params(5, 24),
         name="residual_exchange",
     )(terms, first, *shards)
 
 
-def backward_kernel(length, terms, second, per_token, up_term, packet, g_out, up_grad, packets, up_buf, *scratch):
+def backward_kernel(info, terms, second, per_token, up_term, packet, g_out, up_grad, packets, up_buf, *scratch):
     me, y, c, up, dn, op, oc = ring_places()
     plane = Plane([packet, up_term], [packets, up_buf], *scratch[11:], True)
     grad = pair_sum_to_owner(plane, terms, *scratch[:9])
-    live = (y * 2 + c) * 128 + lax.broadcasted_iota(jnp.int32, (128, 1), 0) < length[0]
+    live = (y * 2 + c) * 128 + lax.broadcasted_iota(jnp.int32, (128, 1), 0) < info[1:2, 0:1]
     g_third = jnp.where(live, per_token[...], 0.0)
     g_out[y, c] = (g_third + normalize_back(second[...].astype(F32), grad)).astype(BF16)
     to_all(g_out, *scratch[9:11])
@@ -498,7 +567,7 @@
     up_grad[...] = total_of(up_buf)
 
 
-def backward(length, terms, second, per_token, up_term, packet):
+def backward(info, terms, second, per_token, up_term, packet):
     return pl.pallas_call(
         backward_kernel,
         out_shape=[
@@ -506,12 +575,12 @@
             jax.ShapeDtypeStruct((64, 512), F32),
             gathered(packet),
         ],
-        in_specs=[SM] + [VM] * 5,
+        in_specs=[VM] * 6,
         out_specs=[VM] * 3,
         scratch_shapes=[pltpu.VMEM((16, 64, 512), BF16), *PAIR_SCRATCH],
-        compiler_params=params(6),
+        compiler_params=params(6, 24),
         name="backward_exchange",
-    )(length, terms, second, per_token, up_term, packet)
+    )(info, terms, second, per_token, up_term, packet)
 
 
 PACKET = 512 + 1024 + 1024 + 128 + 128
@@ -521,7 +590,7 @@
 
 
 def ffn_kernel(
-    length, label, normed, second, up_w, down_w, head_w, per_token_out, packet_out, terms, up_term,
+    info, normed, second, up_w, down_w, head_w, per_token_out, packet_out, terms, up_term,
     slope, g_pre, parts, send, recv,
 ):
     me, y, c, up, dn, op, oc = ring_places()
@@ -534,8 +603,10 @@
     for k, e in peers:
         signal(device(4 - k if k else 0, e))
 
+    length, label = info[1:2, 0:1], info[2:3, 0:1]
+
     def live(start, size):
-        return start + lax.broadcasted_iota(jnp.int32, (size, 1), 0) < length[0]
+        return start + lax.broadcasted_iota(jnp.int32, (size, 1), 0) < length
 
     hidden_sum = jnp.zeros((1, 512), F32)
     for block in range(1024 // ROWS):
@@ -563,13 +634,13 @@
     pooled = parts[0]
     for s in range(1, 8):
         pooled = pooled + parts[s]
-    count = length[0].astype(F32)
+    count = length.astype(F32)
     pooled = pooled / count
     final = normalize(pooled)
     logits = jnp.sum(jnp.dot(thirds(final), head_w[...], preferred_element_type=F32), axis=0, keepdims=True)
     top = jnp.max(logits, axis=-1, keepdims=True)
     total = jnp.log(jnp.sum(jnp.exp(logits - top), axis=-1, keepdims=True)) + top
-    labels = (lax.broadcasted_iota(jnp.int32, logits.shape, 1) == label[0]).astype(F32)
+    labels = (lax.broadcasted_iota(jnp.int32, logits.shape, 1) == label).astype(F32)
     loss = total - jnp.sum(logits * labels, axis=-1, keepdims=True)
     g_logits = (jnp.exp(logits - total) - labels) / 16.0
     g_final = lax.dot_general(thirds(g_logits), head_w[...], RHS_T, preferred_element_type=F32)
@@ -595,7 +666,7 @@
     packet_out[:, 2688:2816] = jnp.broadcast_to(loss, (1, 128))
 
 
-def ffn(length, label, normed, second, up_w, down_w, head_w):
+def ffn(info, normed, second, up_w, down_w, head_w):
     return pl.pallas_call(
         ffn_kernel,
         out_shape=[
@@ -604,7 +675,7 @@
             jax.ShapeDtypeStruct((1024, 1024), BF16),
             jax.ShapeDtypeStruct((1024, 512), BF16),
         ],
-        in_specs=[SM, SM, VM, VM, VM, VM, VM],
+        in_specs=[VM] * 6,
         out_specs=[VM, VM, VM, VM],
         scratch_shapes=[
             pltpu.VMEM((1024, 512), F32),
@@ -613,9 +684,9 @@
             pltpu.SemaphoreType.DMA((4, 2)),
             pltpu.SemaphoreType.DMA((4, 2)),
         ],
-        compiler_params=params(7),
+        compiler_params=params(7, 32),
         name="ffn",
-    )(length, label, normed, second, up_w, down_w, head_w)
+    )(info, normed, second, up_w, down_w, head_w)
 
 
 SCALE = 0.125
@@ -632,7 +703,7 @@
     return jnp.where((cols >= 64) == (head == 1), value, jnp.zeros_like(value))
 
 
-def attend_kernel(length, normed, qkv_w, out_w, qkv, context_t, probs_t, terms):
+def attend_kernel(info, normed, qkv_w, out_w, qkv, context_t, probs_t, terms):
     for block in range(4):
         rows = pl.ds(block * 256, 256)
         qkv[rows] = jnp.dot(normed[rows], qkv_w[...], preferred_element_type=F32).astype(BF16)
@@ -640,7 +711,7 @@
     query_t = (qkv[:, 0:128] * SCALE).T
     values_t = qkv[:, 256:384].T
     out_t = out_w[...].T
-    seen = lax.broadcasted_iota(jnp.int32, (1024, WIDE), 0) < length[0]
+    seen = lax.broadcasted_iota(jnp.int32, (1024, WIDE), 0) < info[1:2, 0:1]
     for block in range(1024 // WIDE):
         cols = slice(block * WIDE, (block + 1) * WIDE)
         for head in range(2):
@@ -654,7 +725,7 @@
         terms[cols] = jnp.dot(context_t[:, cols].T, out_t, preferred_element_type=F32).astype(BF16)
 
 
-def attend(length, normed, qkv_w, out_w):
+def attend(info, normed, qkv_w, out_w):
     return pl.pallas_call(
         attend_kernel,
         out_shape=[
@@ -663,11 +734,11 @@
             jax.ShapeDtypeStruct((2, 1024, 1024), BF16),
             jax.ShapeDtypeStruct((1024, 1024), BF16),
         ],
-        in_specs=[SM, VM, VM, VM],
+        in_specs=[VM] * 4,
         out_specs=[VM] * 4,
-        compiler_params=pltpu.CompilerParams(vmem_limit_bytes=48 * 2**20),
+        compiler_params=pltpu.CompilerParams(vmem_limit_bytes=32 * 2**20),
         name="attend",
-    )(length, normed, qkv_w, out_w)
+    )(info, normed, qkv_w, out_w)
 
 
 def attend_back_kernel(
@@ -722,45 +793,28 @@
             pltpu.VMEM((1024, 128), F32),
             pltpu.VMEM((1024, 128), F32),
         ],
-        compiler_params=pltpu.CompilerParams(vmem_limit_bytes=48 * 2**20),
+        compiler_params=pltpu.CompilerParams(vmem_limit_bytes=32 * 2**20),
         name="attend_back",
     )(g_second, normed, out_w, qkv, probs_t, context_t)
 
 
 def per_device(token_ids, lengths, teacher_bins, table, qkv_shard, out_shard, up_shard, down_shard, head_shard):
-    me = where_am_i()
-    vocab = table.shape[0]
-
-    packet = jnp.concatenate(
-        [
-            token_ids,
-            jnp.broadcast_to(lengths[:, None], (1, 128)),
-            jnp.broadcast_to(teacher_bins[:, None], (1, 128)),
-            jnp.zeros((5, 128), jnp.int32),
-        ],
-        axis=0,
-    )
-    got = spread_ids(packet)
-    length = got[0, 0, 1, 0:1]
-    label = got[0, 0, 2, 0:1]
-    shifted = got[:, :, 0, :] - (me["y"] * 2 + me["xh"]) * vocab
-    inside = (shifted >= 0) & (shifted < vocab)
-    rows = jnp.take(table, jnp.clip(shifted, 0, vocab - 1), axis=0)
-    rows = jnp.where(inside[..., None], rows, jnp.zeros_like(rows))
-    first, normed, qkv_w, out_w, head_w = embed(rows, [qkv_shard.reshape(64, 384), out_shard.T, head_shard])
+    info, first, normed, qkv_w, out_w, head_w = embed(
+        lengths, teacher_bins, token_ids, table, [qkv_shard.reshape(64, 384), out_shard.T, head_shard]
+    )
+    normed = normed.reshape(1024, 1024)
     qkv_w = qkv_w.reshape(1024, 384)
     out_w = out_w.reshape(1024, 128)
     head_w = head_w.reshape(1024, 128)
-    normed = normed.reshape(1024, 1024)
-    qkv, context_t, probs_t, terms = attend(length, normed, qkv_w, out_w)
+    qkv, context_t, probs_t, terms = attend(info, normed, qkv_w, out_w)
     second, normed_two, up_w, down_w = residual(terms.reshape(4, 2, 128, 1024), first, [up_shard, down_shard.T])
     up_w = up_w.reshape(1024, 512)
     down_w = down_w.reshape(1024, 512)
     per_token, packet, terms, up_term = ffn(
-        length, label, normed_two.reshape(1024, 1024), second, up_w, down_w, head_w
+        info, normed_two.reshape(1024, 1024), second, up_w, down_w, head_w
     )
     g_second, up_grad, packets = backward(
-        length, terms.reshape(4, 2, 128, 1024), second, per_token, up_term.reshape(16, 64, 512), packet
+        info, terms.reshape(4, 2, 128, 1024), second, per_token, up_term.reshape(16, 64, 512), packet
     )
     out_term, qkv_term = attend_back(g_second.reshape(1024, 1024), normed, out_w, qkv, probs_t, context_t)
     out_grad, qkv_grad, down_grad, head_grad, loss = collect(

time: 227 us -> 176 us (0.78)
  Pallas kernels: 191 us -> 164 us
  local copies, waits for them, and re-layouts: 26.2 us -> 8.65 us
  other arithmetic: 4.43 us -> 0 us
    gather x1 -> x0, local copies, waits for them, and re-layouts: 9.2 us -> none  [per_device(): rows = jnp.take(table, jnp.clip(shifted, 0, vocab - 1), axis=0)]
    unnamed x25 -> x20, local copies, waits for them, and re-layouts: 14.9 us -> 8.64 us
    pallas_call x1, Pallas kernels: 16.2 us -> 10.2 us  [ffn(): pl.pallas_call(ffn_kernel, out_shape=[jax.ShapeDtypeStruct((1, 1024), F32...]
    pallas_call x1, Pallas kernels: 37.2 us -> 31.9 us  [backward(): pl.pallas_call(backward_kernel, out_shape=[jax.ShapeDtypeStruct((4, 2, 12...]
    pallas_call x1, Pallas kernels: 35.3 us -> 31.3 us  [residual(): pl.pallas_call(residual_kernel, out_shape=[jax.ShapeDtypeStruct((128, 102...]
    pallas_call x1, Pallas kernels: 13.1 us -> 9.64 us  [attend(): pl.pallas_call(attend_kernel, out_shape=[jax.ShapeDtypeStruct((1024, 384)...]
    pallas_call x1, Pallas kernels: 20.7 us -> 17.8 us  [collect(): pl.pallas_call(collect_kernel, out_shape=[jax.ShapeDtypeStruct((64, 128),...]
    pallas_call x2 -> x1, Pallas kernels: 58.3 us -> 55.3 us  [embed(): pl.pallas_call(embed_kernel, out_shape=[jax.ShapeDtypeStruct((8, 128), jn...]
where the time goes in v3:
time: 176 us
  Pallas kernels  164 us (93%)
  local copies, waits for them, and re-layouts  8.65 us (5%)
  between operations  3.23 us (2%)
    pallas_call x1, Pallas kernels, embed(): pl.pallas_call(embed_kernel, out_shape=[jax.ShapeDtypeStruct((8, 128), jn...  55.3 us
    pallas_call x1, Pallas kernels, backward(): pl.pallas_call(backward_kernel, out_shape=[jax.ShapeDtypeStruct((4, 2, 12...  31.9 us
    pallas_call x1, Pallas kernels, residual(): pl.pallas_call(residual_kernel, out_shape=[jax.ShapeDtypeStruct((128, 102...  31.3 us
    pallas_call x1, Pallas kernels, collect(): pl.pallas_call(collect_kernel, out_shape=[jax.ShapeDtypeStruct((64, 128),...  17.8 us
    pallas_call x1, Pallas kernels, ffn(): pl.pallas_call(ffn_kernel, out_shape=[jax.ShapeDtypeStruct((1, 1024), F32...  10.2 us
    pallas_call x1, Pallas kernels, attend(): pl.pallas_call(attend_kernel, out_shape=[jax.ShapeDtypeStruct((1024, 384)...  9.64 us
    unnamed x20, local copies, waits for them, and re-layouts  8.64 us
    pallas_call x1, Pallas kernels, attend_back(): pl.pallas_call(attend_back_kernel, out_shape=[jax.ShapeDtypeStruct((1024,...  7.71 us

profile of v3, /device:TPU:1, one launch (start us, length us, event | category | flops | bytes accessed | tf_op | source)
XLA Modules:
  0.0 175.7 jit_solution(8205270923120662955)
XLA Ops:
  0.6 0.0 copy-start
  1.9 0.0 copy-done
  2.0 0.0 copy-start.1
  2.0 3.2 %copy-done.1 = bf16[3816,1024]{1,0:T(8,128)(2,1)S(1)} copy-done((bf16[3816,1024]{1,0:T(8,128)(2,1)S(1)}, bf16[3816,1024]{1,0:T(8,128)(2,1)}, u32[]{:S(2)}) %copy-start.1) | copy-done | bytes 7815192
  5.2 0.0 copy-start.4
  5.2 0.7 copy-done.4
  5.9 0.7 copy-done.5
  6.6 0.7 copy-done.6
  7.3 55.3 %embed_exchange.1 = (s32[8,128]{1,0:T(8,128)S(1)}, bf16[128,1024]{1,0:T(8,128)(2,1)S(1)}, bf16[4,2,128,1024]{3,2,1,0:T(8,128)(2,1)S(1)}, bf16[16,64,384]{2,1,0:T...) custom-call(s32[1]{0:T(128)S(6)} %copy.30.count, s32[1]{0:T(128)S(6)} %copy.31.label, ...), custom_call_target="tpu_custom_call" | custom-call | tf_op jit(solution)/shard_map/embed_exchange/pallas_call | solution.py:451
  62.6 0.0 copy-start.2
  62.6 0.0 copy-start.3
  62.7 9.6 %attend.1 = (bf16[1024,384]{1,0:T(8,128)(2,1)S(1)}, bf16[128,1024]{1,0:T(8,128)(2,1)S(1)}, bf16[2,1024,1024]{2,1,0:T(8,128)(2,1)S(1)}, bf16[1024,1024]{1,0:T(8,128)(2,1)S(1)}) custom-call(s32[8,128]{1,0:T(8,128)S(1)} %get-tuple-element.34.info, bf16[1024,1024]{1,0:T(8,128)(2,1)S(1)} %bitcast.26, bf16[1024,384]{1,0:T(8,128)(2,1)S(1)} %bitcast.38, ...), custom_call_target="tpu_custom_call" | custom-call | tf_op jit(solution)/shard_map/attend/pallas_call | solution.py:729
  72.3 0.0 copy-done.2
  72.3 0.0 copy-done.3
  72.3 31.3 %residual_exchange.1 = (bf16[128,1024]{1,0:T(8,128)(2,1)S(1)}, bf16[4,2,128,1024]{3,2,1,0:T(8,128)(2,1)S(1)}, bf16[16,64,512]{2,1,0:T(8,128)(2,1)S(1)}, bf16[16,64,512]{2,1,0:T(8,128)(2,1)S(1)}) custom-call(bf16[4,2,128,1024]{3,2,1,0:T(8,128)(2,1)S(1)} %bitcast.29, bf16[128,1024]{1,0:T(8,128)(2,1)S(1)} %get-tuple-element.39.first, ...), custom_call_target="tpu_custom_call" | custom-call | tf_op jit(solution)/shard_map/residual_exchange/pallas_call | solution.py:542
  103.6 10.2 %ffn.1 = (f32[1,1024]{1,0:T(1,128)S(1)}, f32[1,2816]{1,0:T(1,128)S(1)}, bf16[1024,1024]{1,0:T(8,128)(2,1)S(1)}, bf16[1024,512]{1,0:T(8,128)(2,1)S(1)}) custom-call(s32[8,128]{1,0:T(8,128)S(1)} %get-tuple-element.34.info, bf16[1024,1024]{1,0:T(8,128)(2,1)S(1)} %bitcast.31, bf16[128,1024]{1,0:T(8,128)(2,1)S(1)} %get-tuple-element.41.second, ...), custom_call_target="tpu_custom_call" | custom-call | tf_op jit(solution)/shard_map/ffn/pallas_call | solution.py:670
  113.8 31.9 %backward_exchange.1 = (bf16[4,2,128,1024]{3,2,1,0:T(8,128)(2,1)S(1)}, f32[64,512]{1,0:T(8,128)S(1)}, f32[16,1,2816]{2,1,0:T(1,128)S(1)}) custom-call(s32[8,128]{1,0:T(8,128)S(1)} %get-tuple-element.34.info, bf16[4,2,128,1024]{3,2,1,0:T(8,128)(2,1)S(1)} %bitcast.30, bf16[128,1024]{1,0:T(8,128)(2,1)S(1)} %get-tuple-element.41.second, ...), custom_call_target="tpu_custom_call" | custom-call | tf_op jit(solution)/shard_map/backward_exchange/pallas_call | solution.py:571
  145.8 7.7 %attend_back.1 = (bf16[1024,128]{1,0:T(8,128)(2,1)S(1)}, bf16[1024,384]{1,0:T(8,128)(2,1)S(1)}) custom-call(bf16[1024,1024]{1,0:T(8,128)(2,1)S(1)} %bitcast.28, bf16[1024,1024]{1,0:T(8,128)(2,1)S(1)} %bitcast.27, bf16[1024,128]{1,0:T(8,128)(2,1)S(1)} %bitcast.33, bf16[1024,384]{1,0:T(8,128)(2,1)S(1)} %get-tuple-element.51.qkv, ...), custom_call_target="tpu_custom_call" | custom-call | tf_op jit(solution)/shard_map/attend_back/pallas_call | solution.py:781
  153.5 17.8 %collect_gradients.1 = (f32[64,128]{1,0:T(8,128)S(1)}, f32[64,3,128]{2,1,0:T(4,128)S(1)}, f32[512,64]{1,0:T(8,128)S(1)}, f32[64,128]{1,0:T(8,128)S(1)}, f32[1,128]{1,0:T(1,128)S(1)}) custom-call(f32[16,2816]{1,0:T(8,128)S(1)} %bitcast.39, bf16[16,64,128]{2,1,0:T(8,128)(2,1)S(1)} %bitcast.40, bf16[16,64,384]{2,1,0:T(8,128)(2,1)S(1)} %bitcast.37), custom_call_target="tpu_custom_call" | custom-call | tf_op jit(solution)/shard_map/collect_gradients/pallas_call | solution.py:276
  171.2 0.6 copy.19
  171.9 0.8 copy.20
  172.7 0.6 copy.33
  173.3 0.7 copy.34
  174.0 0.6 copy.35
  (4 shorter events, 0.0 us)
Async XLA Ops:
  0.6 1.3 copy-start
  2.0 3.2 %copy-start.1 = (bf16[3816,1024]{1,0:T(8,128)(2,1)S(1)}, bf16[3816,1024]{1,0:T(8,128)(2,1)}, u32[]{:S(2)}) copy-start(bf16[3816,1024]{1,0:T(8,128)(2,1)} %table.1) | copy-start | bytes 23445508
  5.2 0.7 copy-start.4
  5.9 0.7 copy-start.5
  6.6 0.7 copy-start.6
  62.6 9.7 %copy-start.2 = (bf16[64,512]{1,0:T(8,128)(2,1)S(1)}, bf16[64,512]{1,0:T(8,128)(2,1)}, u32[]{:S(2)}) copy-start(bf16[64,512]{1,0:T(8,128)(2,1)} %up_s.1) | copy-start | bytes 196612
  62.6 9.7 %copy-start.3 = (bf16[512,64]{0,1:T(8,128)(2,1)S(1)}, bf16[512,64]{0,1:T(8,128)(2,1)}, u32[]{:S(2)}) copy-start(bf16[512,64]{0,1:T(8,128)(2,1)} %param.16) | copy-start | bytes 196612
